TPU v7x, 32 devices: a whole 2x2x4 slice. The times are simulated.
32 devices in a mesh: gx: 4 (over y, x), gy: 2 (over core), gz: 4 (over z).
Axes of the slice: x: 2, y: 2, z: 4, core: 2. Of those that a mesh axis runs over, the one named last changes fastest.
Arguments:
- data: float32 [128, 64, 512], P('gx', 'gy', 'gz'), may hold values from -120 to 120
- weights: float32 [8, 512], P(None, 'gz'), may hold values from -3 to 3
Outputs:
- solution: float32 [128, 64, 512], P('gx', 'gy', 'gz')
- residual: float32 [128, 64, 512], P('gx', 'gy', 'gz')
- norms: float32 [4], replicated
All inputs are finite; a program needn't handle non-finite values.
Results may differ from a plain program's by a relative error of at most 0.0001.
Values sent between devices are 32-bit elements; how exact they have to be, the bound alone decides.
A program may use at most 128 MiB of HBM per device.

v0:
```python
import functools
import jax
import jax.numpy as jnp
from jax import lax
from jax.experimental import pallas as pl
from jax.experimental.pallas import tpu as pltpu
from jax.sharding import PartitionSpec as P

HALF = 4
RELAX = 0.45
F32 = jnp.float32
BF16 = jnp.bfloat16
HX = (4, 6)
OFFSETS = [j - HALF for j in range(HALF)] + [j - HALF + 1 for j in range(HALF, 2 * HALF)]


def iota(shape, dim):
    return lax.broadcasted_iota(jnp.int32, shape, dim)


def cyclic(index, size, own):
    cut = (size + own) // 2
    return jnp.where(index < cut, index, index - size)


def split(x):
    high = x.astype(BF16)
    return high, (x - high.astype(F32)).astype(BF16)


def dot(a, b):
    return lax.dot_general(a, b, (((1,), (0,)), ((), ())), preferred_element_type=F32)


def dot3(x, mh, ml):
    h, l = split(x)
    return dot(h, mh) + dot(h, ml) + dot(l, mh)


def dot2(x, m):
    h, l = split(x)
    return dot(h, m) + dot(l, m)


def dot2l(m, x):
    h, l = split(x)
    return dot(m, h) + dot(m, l)


def restrict_matrix(fine, coarse, axis):
    k = fine - 2 * coarse + 1
    m = jnp.where((k == 0) | (k == 3), 0.125, jnp.where((k == 1) | (k == 2), 0.375, 0.0))
    return m.astype(F32)


def prolong_matrix(fine, coarse, limit):
    centre = fine >> 1
    other = jnp.where((fine & 1) == 1, centre + 1, centre - 1)
    m = jnp.where(coarse == centre, 0.75, jnp.where(coarse == other, 0.25, 0.0))
    return jnp.where((fine >= 0) & (fine < limit), m, 0.0).astype(F32)


def build_matrices(nz, whole, wall, *outs):
    z0 = lax.axis_index("gz") * nz
    for level in range(4):
        own = nz >> level
        total = whole >> level
        size = 2 * nz if level < 2 else total
        base = z0 >> level if level < 2 else 0

        def place(index):
            return cyclic(index, size, own) if level < 2 else index

        g = iota((whole, size), 0) >> level
        p = place(iota((whole, size), 1)) + base
        pick = jnp.where(g == p, 0.5**level, 0.0).astype(F32)
        w = lax.dot_general(
            wall, pick, (((1,), (0,)), ((), ())),
            preferred_element_type=F32, precision=lax.Precision.HIGHEST,
        )
        pr = place(iota((size, size), 0))
        pc = place(iota((size, size), 1))
        ok = (pr + base >= 0) & (pr + base < total) & (pc + base >= 0) & (pc + base < total)
        diff = pr - pc
        at = jnp.where(diff == 0, 1.0, 0.0).astype(F32)
        for j, offset in enumerate(OFFSETS):
            at = at + jnp.where(diff == offset, w[j : j + 1, :], 0.0)
        at = jnp.where(ok, at, 0.0)
        a = at.T
        stiff = 0.25**level
        m = lax.dot_general(
            at, a, (((1,), (0,)), ((), ())),
            preferred_element_type=F32, precision=lax.Precision.HIGHEST,
        )
        lap = jnp.where(diff == 0, 6.0, jnp.where((diff == 1) | (diff == -1), -1.0, 0.0))
        m = m + jnp.where(ok, stiff * lap, 0.0)
        d = jnp.sum(jnp.where(diff == 0, m, 0.0), axis=0, keepdims=True)
        col = place(iota((1, size), 1)) + base
        inside = (col >= 0) & (col < total)
        safe = jnp.where(inside, d, 1.0)
        c = jnp.where(inside, RELAX / safe, 0.0)
        inv = jnp.where(inside, safe * (1.0 / RELAX), 0.0)
        mh, ml = split(m * c)
        o = outs[3 * level : 3 * level + 3]
        o[0][...] = mh
        o[1][...] = ml
        o[2][0:1, :] = c
        o[2][1:2, :] = inv
        if level == 0:
            ah, al = split(a)
            outs[12][...] = ah
            outs[13][...] = al


def chunk_of(count, rows, most):
    best = 1
    for planes in range(1, count + 1):
        if count % planes == 0 and planes * rows <= most:
            best = planes
    return best


def sweep(src, r_at, emit, first, count, stiff, mats, xmask, ymask, init=None, own=None, most=800):
    mh, ml, cv = mats
    rows, size = src.shape[1], src.shape[2]
    planes = chunk_of(count, rows, most)
    keep, lanes = own or (rows, size)
    c = cv[0:1, 0:lanes]
    inv = cv[1:2, 0:lanes]
    yi = iota((rows, lanes), 0)

    def step(k, carry):
        x0 = first + k * planes
        u = src[pl.ds(x0, planes), 0:keep, :]
        um = dot3(u.reshape(planes * keep, size), mh[:, 0:lanes], ml[:, 0:lanes])
        for p in range(planes):
            x = x0 + p
            uc = src[x, :, 0:lanes]
            low = pltpu.roll(uc, 1, 0)
            high = pltpu.roll(uc, rows - 1, 0)
            if ymask is None:
                low = jnp.where(yi == 0, 0.0, low)
                high = jnp.where(yi == rows - 1, 0.0, high)
            side = src[x - 1, 0:keep, 0:lanes] + src[x + 1, 0:keep, 0:lanes]
            nb = side + (low + high)[0:keep]
            if ymask is None:
                nb = nb * stiff
            else:
                nb = nb * (ymask[0:keep, 0:lanes] * (xmask(x) * stiff))
            delta = c * (r_at(x)[0:keep, 0:lanes] + nb) - um[p * keep : (p + 1) * keep]
            carry = emit(x, uc[0:keep], delta, inv, carry)
        return carry

    return lax.fori_loop(0, count // planes, step, init)


def restrict(gz, first, count, ry, out, lanes):
    group = chunk_of(count, 1, 8)

    def step(k, carry):
        values = []
        for j in range(group):
            x = first + 2 * (k * group + j)
            t = (gz[x - 1] + 3.0 * gz[x] + 3.0 * gz[x + 1] + gz[x + 2]) * 0.125
            values.append(dot2l(ry, t))
        for j in range(group):
            out(k * group + j, values[j])
        return carry

    lax.fori_loop(0, count // group, step, 0)


def inside_mask(base, limit, pad):
    def mask(x):
        g = base + x - pad
        return jnp.where((g >= 0) & (g < limit), 1.0, 0.0).astype(F32)

    return mask


def y_mask(rows, size, own, base, limit):
    y = cyclic(iota((rows, size), 0), rows, own) + base
    return jnp.where((y >= 0) & (y < limit), 1.0, 0.0).astype(F32)


def zero_planes(ref, *planes):
    for x in planes:
        ref[x] = jnp.zeros(ref.shape[1:], F32)


def geometry(level, dims):
    nx, ny, nz = (v >> level for v in dims)
    gx, gy = lax.axis_size("gx"), lax.axis_size("gy")
    return dict(
        nx=nx, ny=ny, nz=nz, x0=lax.axis_index("gx") * nx, y0=lax.axis_index("gy") * ny,
        z0=lax.axis_index("gz") * nz, NX=nx * gx, NY=ny * gy, NZ=nz * lax.axis_size("gz"),
    )


def down_kernel(level, dims, *refs):
    if level == 0:
        ext, ah, al, mh, ml, cv, rhs, eb, r_next, part, ua, gz = refs
    else:
        rhs, mh, ml, cv, eb, r_next, part, ua, gz = refs
    geo = geometry(level, dims)
    nx, ny, nz = geo["nx"], geo["ny"], geo["nz"]
    hx = HX[level]
    count = nx + 2 * hx
    rows, size = ua.shape[1], ua.shape[2]
    pad = hx + 1
    c = cv[0:1, :]
    zero_planes(ua, 0, count + 1)
    reach = hx - 1 - level
    zero_planes(eb, *range(pad - reach), *range(pad + nx + reach, count + 2))
    if level == 0:
        planes = chunk_of(count, rows, 448)

        def first(k, carry):
            x0 = k * planes
            r = dot3(ext[pl.ds(x0, planes)].reshape(planes * rows, size), ah[...], al[...])
            for p in range(planes):
                rp = r[p * rows : (p + 1) * rows]
                rhs[x0 + p] = rp
                ua[x0 + p + 1] = c * rp
            return carry

        lax.fori_loop(0, count // planes, first, 0)
    else:

        def first(x, carry):
            ua[x + 1] = c * rhs[x]
            return carry

        lax.fori_loop(0, count, first, 0)
    xmask = inside_mask(geo["x0"], geo["NX"], pad)
    ymask = y_mask(rows, size, ny, geo["y0"], geo["NY"])
    mats = (mh, ml, cv)
    stiff = 0.25**level

    def r_at(x):
        return rhs[x - 1]

    def keep(x, u, delta, inv, carry):
        eb[x] = u + delta
        return carry

    sweep(ua, r_at, keep, pad - reach, nx + 2 * reach, stiff, mats, xmask, ymask, 0)
    lanes = gz.shape[2]
    fine = cyclic(iota((size, lanes), 0), size, nz)
    coarse = iota((size, lanes), 1)
    rz = jnp.where(coarse < nz // 2, restrict_matrix(fine, coarse, 0), 0.0).astype(BF16)
    ry = restrict_matrix(
        cyclic(iota((ny // 2, rows), 1), rows, ny), iota((ny // 2, rows), 0), 1
    ).astype(BF16)

    def defect(x, u, delta, inv, carry):
        g = delta * inv
        gz[x] = dot2(g, rz)
        mine = g[0:ny, 0:nz]
        return carry + mine * mine * jnp.where((x >= pad) & (x < pad + nx), 1.0, 0.0).astype(F32)

    total = sweep(
        eb, r_at, defect, pad - 1, nx + 2, stiff, mats, xmask, ymask, jnp.zeros((ny, nz), F32)
    )
    part[...] = jnp.full(part.shape, jnp.sum(total), F32)

    def put(i, value):
        r_next[i] = value

    restrict(gz, pad, nx // 2, ry, put, lanes)


def prolong_into(coarse_ref, coarse_first, coarse_count, pz, py, buf, error, dst, xmask):
    group = chunk_of(coarse_count, 1, 11)
    rows, size = coarse_ref.shape[1:]

    def step(k, carry):
        z = coarse_ref[pl.ds(coarse_first + k * group, group)]
        z = dot2(z.reshape(group * rows, size), pz)
        values = [dot2l(py, z[j * rows : (j + 1) * rows]) for j in range(group)]
        for j in range(group):
            buf[k * group + j] = values[j]
        return carry

    lax.fori_loop(0, coarse_count // group, step, 0)

    def join(i, carry):
        x = 1 + 2 * (i - 1)
        mid = 0.75 * buf[i]
        dst[x] = error(x) + xmask(x) * (mid + 0.25 * buf[i - 1])
        dst[x + 1] = error(x + 1) + xmask(x + 1) * (mid + 0.25 * buf[i + 1])
        return carry

    lax.fori_loop(1, coarse_count - 1, join, 0)


def coarse_kernel(dims, r2, m2h, m2l, c2, m3h, m3l, c3, u2, part, ua, ub, gz, r3, e3a, e3b, buf):
    g2 = geometry(2, dims)
    g3 = geometry(3, dims)
    N2, N3 = g2["NX"], g3["NX"]
    pad = 4
    one = lambda x: 1.0
    for ref in (ua, ub):
        zero_planes(ref, 0, N2 + 1)
    zero_planes(e3a, 0, N3 + 1)
    zero_planes(e3b, 0, N3 + 1)
    zero_planes(gz, 0, N2 + 1)
    zero_planes(u2, *range(pad), *range(N2 + pad, N2 + 2 * pad))
    mats2, mats3 = (m2h, m2l, c2), (m3h, m3l, c3)
    cc = c2[0:1, :]

    def first(x, carry):
        ua[x + 1] = cc * r2[x]
        return carry

    lax.fori_loop(0, N2, first, 0)
    r_at = lambda x: r2[x - 1]

    def into(ref, shift=0):
        def emit(x, u, delta, inv, carry):
            ref[x + shift] = u + delta
            return carry

        return emit

    s2, s3 = 0.25**2, 0.25**3
    sweep(ua, r_at, into(ub), 1, N2, s2, mats2, one, None, 0)
    NY2, NZ2, NY3, NZ3 = g2["NY"], g2["NZ"], g3["NY"], g3["NZ"]
    rz = restrict_matrix(iota((NZ2, NZ3), 0), iota((NZ2, NZ3), 1), 0).astype(BF16)
    ry = restrict_matrix(iota((NY3, NY2), 1), iota((NY3, NY2), 0), 1).astype(BF16)

    def defect(x, u, delta, inv, carry):
        g = delta * inv
        gz[x] = dot2(g, rz)
        return carry + g * g

    total = sweep(ub, r_at, defect, 1, N2, s2, mats2, one, None, jnp.zeros((NY2, NZ2), F32))
    part[...] = jnp.full(part.shape, jnp.sum(total), F32)
    c3v = c3[0:1, :]

    def put(i, value):
        r3[i] = value
        e3a[i + 1] = c3v * value

    restrict(gz, 1, N3, ry, put, NZ3)
    sweep(e3a, lambda x: r3[x - 1], into(e3b), 1, N3, s3, mats3, one, None, 0)
    pz = prolong_matrix(iota((NZ3, NZ2), 1), iota((NZ3, NZ2), 0), NZ2).astype(BF16)
    py = prolong_matrix(iota((NY2, NY3), 0), iota((NY2, NY3), 1), NY2).astype(BF16)
    prolong_into(e3b, 0, N3 + 2, pz, py, buf, lambda x: ub[x], ua, one)
    sweep(ua, r_at, into(ub), 1, N2, s2, mats2, one, None, 0)
    sweep(ub, r_at, into(u2, pad - 1), 1, N2, s2, mats2, one, None, 0)


def up_kernel(dims, u2, r1, e1, m1h, m1l, c1, rhs, e0, m0h, m0l, c0, sol, res, part,
              va, vb, vbuf, ua, ub, ubuf):
    g0, g1, g2 = geometry(0, dims), geometry(1, dims), geometry(2, dims)
    rows, size = va.shape[1], va.shape[2]
    count = g1["nx"] + 2 * HX[1]
    zero_planes(va, 0, count + 1)
    zero_planes(vb, 0, count + 1)
    xmask = inside_mask(g1["x0"], g1["NX"], HX[1] + 1)
    ymask = y_mask(rows, size, g1["ny"], g1["y0"], g1["NY"])
    NY2, NZ2 = g2["NY"], g2["NZ"]
    pz = prolong_matrix(
        cyclic(iota((NZ2, size), 1), size, g1["nz"]) + g1["z0"], iota((NZ2, size), 0), g1["NZ"]
    ).astype(BF16)
    py = prolong_matrix(
        cyclic(iota((rows, NY2), 0), rows, g1["ny"]) + g1["y0"], iota((rows, NY2), 1), g1["NY"]
    ).astype(BF16)
    first = g2["x0"] + 4 - HX[1] // 2 - 1
    prolong_into(u2, first, count // 2 + 2, pz, py, vbuf, lambda x: e1[x], va, xmask)
    mats = (m1h, m1l, c1)

    def into(ref):
        def emit(x, u, delta, inv, carry):
            ref[x] = u + delta
            return carry

        return emit

    r1_at = lambda x: r1[x - 1]
    q, n1 = HX[1] + 1, g1["nx"]
    sweep(va, r1_at, into(vb), q - 3, n1 + 6, 0.25, mats, xmask, ymask, 0)
    sweep(vb, r1_at, into(va), q - 2, n1 + 4, 0.25, mats, xmask, ymask, 0)
    rows0, size0 = ua.shape[1], ua.shape[2]
    count0 = g0["nx"] + 2 * HX[0]
    nx, ny, nz = g0["nx"], g0["ny"], g0["nz"]
    pad = HX[0] + 1
    zero_planes(ua, 0, count0 + 1)
    zero_planes(ub, 0, count0 + 1)
    xmask0 = inside_mask(g0["x0"], g0["NX"], pad)
    ymask0 = y_mask(rows0, size0, ny, g0["y0"], g0["NY"])
    pz = prolong_matrix(
        cyclic(iota((size, size0), 1), size0, nz) + g0["z0"],
        cyclic(iota((size, size0), 0), size, g1["nz"]) + g1["z0"], g0["NZ"],
    ).astype(BF16)
    py = prolong_matrix(
        cyclic(iota((rows0, rows), 0), rows0, ny) + g0["y0"],
        cyclic(iota((rows0, rows), 1), rows, g1["ny"]) + g1["y0"], g0["NY"],
    ).astype(BF16)
    first = HX[1] + 1 - HX[0] // 2 - 1
    prolong_into(va, first, count0 // 2 + 2, pz, py, ubuf, lambda x: e0[x], ua, xmask0)
    mats0 = (m0h, m0l, c0)
    r0_at = lambda x: rhs[x - 1]
    sweep(ua, r0_at, into(ub), pad - 2, nx + 4, 1.0, mats0, xmask0, ymask0, 0)
    sweep(ub, r0_at, into(ua), pad - 1, nx + 2, 1.0, mats0, xmask0, ymask0, 0)

    def final(x, u, delta, inv, carry):
        g = delta * inv
        sol[x - pad] = u
        res[x - pad] = g
        return carry + g * g

    total = sweep(
        ua, r0_at, final, pad, nx, 1.0, mats0, xmask0, ymask0, jnp.zeros((ny, nz), F32), (ny, nz)
    )
    part[...] = jnp.full(part.shape, jnp.sum(total), F32)


AXES = ("gx", "gy", "gz")
MESH = pl.DeviceIdType.MESH
WIDTH = 40


class Pair:
    def __init__(self, axis, up, down, sends, recvs, slot):
        n, me = lax.axis_size(axis), lax.axis_index(axis)
        self.has_low, self.has_high = me > 0, me < n - 1

        def copy(refs, k, target):
            return pltpu.make_async_remote_copy(
                src_ref=refs[0], dst_ref=refs[1], send_sem=sends.at[k], recv_sem=recvs.at[k],
                device_id={axis: target}, device_id_type=MESH,
            )

        self.up = copy(up, slot, lax.rem(me + 1, n))
        self.down = copy(down, slot + 1, lax.rem(me + n - 1, n))

    def start(self):
        pl.when(self.has_high)(self.up.start)
        pl.when(self.has_low)(self.down.start)

    def wait(self):
        pl.when(self.has_low)(self.up.wait_recv)
        pl.when(self.has_high)(self.down.wait_recv)

    def sent(self):
        pl.when(self.has_high)(self.up.wait_send)
        pl.when(self.has_low)(self.down.wait_send)

    def clear(self, low, high):
        @pl.when(jnp.logical_not(self.has_low))
        def _():
            low[...] = jnp.zeros(low.shape, F32)

        @pl.when(jnp.logical_not(self.has_high))
        def _():
            high[...] = jnp.zeros(high.shape, F32)


def linear():
    gy, gz = lax.axis_size("gy"), lax.axis_size("gz")
    return (lax.axis_index("gx") * gy + lax.axis_index("gy")) * gz + lax.axis_index("gz")


def coordinates(t):
    gy, gz = lax.axis_size("gy"), lax.axis_size("gz")
    return (t // (gy * gz), lax.rem(t // gz, gy), lax.rem(t, gz))


def device_count():
    return lax.axis_size("gx") * lax.axis_size("gy") * lax.axis_size("gz")


def signal_all():
    n, me = device_count(), linear()
    barrier = pltpu.get_barrier_semaphore()

    def step(k, carry):
        pl.semaphore_signal(
            barrier, inc=1, device_id=coordinates(lax.rem(me + k, n)), device_id_type=MESH
        )
        return carry

    lax.fori_loop(1, n, step, 0)


def wait_all():
    pl.semaphore_wait(pltpu.get_barrier_semaphore(), device_count() - 1)


def everyone(block, buf, sends, recvs):
    n, me = device_count(), linear()

    def copy(k, slot):
        return pltpu.make_async_remote_copy(
            src_ref=block, dst_ref=buf.at[slot], send_sem=sends.at[k], recv_sem=recvs.at[k],
            device_id=coordinates(lax.rem(me + k, n)), device_id_type=MESH,
        )

    def start(k, carry):
        copy(k, me).start()
        return carry

    def wait(k, carry):
        c = copy(k, lax.rem(me + n - k, n))
        c.wait_recv()
        c.wait_send()
        return carry

    lax.fori_loop(1, n, start, 0)
    buf[me] = block[...]
    lax.fori_loop(1, n, wait, 0)


def pack_faces(data, low, high):
    nx, ny, nz = data.shape
    slots = nz // WIDTH
    per = -(-nx // slots)
    rest = jnp.zeros((ny, nz - slots * WIDTH), F32)
    for i in range(per):
        planes = [min(k * per + i, nx - 1) for k in range(slots)]
        low[i] = jnp.concatenate([data[x][:, :WIDTH] for x in planes] + [rest], axis=1)
        high[i] = jnp.concatenate([data[x][:, nz - WIDTH :] for x in planes] + [rest], axis=1)


def unpack_faces(dims, from_low, from_high, ext, pad):
    nx, ny, nz = dims
    slots = nz // WIDTH
    per = -(-nx // slots)
    gap = jnp.zeros((ny, nz - 2 * WIDTH), F32)
    for x in range(nx):
        k, i = x // per, x % per
        part = slice(k * WIDTH, (k + 1) * WIDTH)
        ext[pad + x, 0:ny, nz:] = jnp.concatenate(
            [from_high[i][:, part], gap, from_low[i][:, part]], axis=1
        )


def gather_weights(weights, parts, sends, recvs):
    n, me = lax.axis_size("gz"), lax.axis_index("gz")

    def copy(k, slot):
        return pltpu.make_async_remote_copy(
            src_ref=weights, dst_ref=parts.at[slot], send_sem=sends.at[k], recv_sem=recvs.at[k],
            device_id={"gz": lax.rem(me + k, n)}, device_id_type=MESH,
        )

    for k in range(1, n):
        copy(k, me).start()

    def finish():
        parts[me] = weights[...]
        for k in range(1, n):
            c = copy(k, lax.rem(me + n - k, n))
            c.wait_recv()
            c.wait_send()
        return jnp.concatenate([parts[i] for i in range(n)], axis=1)

    return finish


def whole_kernel(names, dims, data, weights, sol, res, norms, *scratch):
    r = dict(zip(names, scratch))
    nx, ny, nz = dims
    n, gz = device_count(), lax.axis_size("gz")
    ns, nr = r["near_send"], r["near_recv"]
    signal_all()
    pack_faces(data, r["f_low"], r["f_high"])
    ext, hx = r["ext"], HX[0]
    for x in range(nx):
        ext[hx + x, 0:ny, 0:nz] = data[x]
    wait_all()
    finish = gather_weights(weights, r["wparts"], r["w_send"], r["w_recv"])
    faces = Pair("gz", (r["f_high"], r["g_low"]), (r["f_low"], r["g_high"]), ns, nr, 0)
    faces.clear(r["g_low"], r["g_high"])
    faces.start()

    def x_pair(lanes, slot):
        return Pair(
            "gx",
            (ext.at[nx : nx + hx, 0:ny, lanes], ext.at[0:hx, 0:ny, lanes]),
            (ext.at[hx : 2 * hx, 0:ny, lanes], ext.at[nx + hx : nx + 2 * hx, 0:ny, lanes]),
            ns, nr, slot,
        )

    near = x_pair(slice(0, nz), 2)
    near.clear(ext.at[0:hx, 0:ny, :], ext.at[nx + hx : nx + 2 * hx, 0:ny, :])
    near.start()
    level = [[r["m%d%s" % (k, t)] for t in "hlc"] for k in range(4)]
    build_matrices(nz, nz * gz, finish(), *(level[0] + level[1] + level[2] + level[3]), r["ah"], r["al"])
    faces.wait()
    unpack_faces(dims, r["g_low"], r["g_high"], ext, hx)
    far = x_pair(slice(nz, 2 * nz), 4)
    far.start()
    near.wait()
    far.wait()
    ys = Pair("gy", (ext.at[:, ny - 8 : ny, :], r["y_low"]), (ext.at[:, 0:8, :], r["y_high"]), ns, nr, 6)
    ys.clear(r["y_low"], r["y_high"])
    ys.start()
    ys.wait()
    near.sent()
    far.sent()
    faces.sent()
    ys.sent()
    upper = iota((8, 2 * nz), 0) < 4

    def join(x, carry):
        ext[x, ny : ny + 8, :] = jnp.where(upper, r["y_high"][x], r["y_low"][x])
        return carry

    lax.fori_loop(0, nx + 2 * hx, join, 0)
    down_kernel(0, dims, ext, r["ah"], r["al"], *level[0], r["rhs"], r["e0"], r["r1"], r["p0"], r["ua"], r["gz0"])
    n1, m1, k1 = nx // 2, ny // 2, nz // 2
    h1 = HX[1]
    x1, r1, half = r["x1"], r["r1"], n1 // 2
    for a in range(half):
        r["b_own"][a] = jnp.concatenate([r1[a][:, :k1], r1[a + half][:, :k1]], axis=1)
    zs = Pair("gz", (r["b_own"], r["b_low"]), (r["b_own"], r["b_high"]), ns, nr, 8)
    zs.clear(r["b_low"], r["b_high"])
    zs.start()
    zs.wait()
    blank = jnp.zeros((m1, k1), F32)
    for x in range(n1):
        a, part = x % half, slice((x // half) * k1, (x // half + 1) * k1)
        x1[h1 + x, 0:m1, :] = jnp.concatenate(
            [r1[x][:, :k1], r["b_high"][a][:, part], blank, r["b_low"][a][:, part]], axis=1
        )
    xs = Pair(
        "gx",
        (x1.at[n1 : n1 + h1, 0:m1, :], x1.at[0:h1, 0:m1, :]),
        (x1.at[h1 : 2 * h1, 0:m1, :], x1.at[n1 + h1 : n1 + 2 * h1, 0:m1, :]),
        ns, nr, 10,
    )
    xs.clear(x1.at[0:h1, 0:m1, :], x1.at[n1 + h1 : n1 + 2 * h1, 0:m1, :])
    xs.start()
    xs.wait()
    ys = Pair(
        "gy",
        (x1.at[:, m1 - 8 : m1, :], x1.at[:, m1 + 8 : m1 + 16, :]),
        (x1.at[:, 0:8, :], x1.at[:, m1 : m1 + 8, :]),
        ns, nr, 12,
    )
    ys.clear(x1.at[:, m1 + 8 : m1 + 16, :], x1.at[:, m1 : m1 + 8, :])
    ys.start()
    ys.wait()
    zs.sent()
    xs.sent()
    ys.sent()
    down_kernel(1, dims, x1, *level[1], r["e1"], r["r2"], r["p1"], r["va"], r["gz1"])
    n2, m2, k2 = nx // 4, ny // 4, nz // 4
    slots = nz // k2
    per = n2 // slots
    for a in range(per):
        r["c_own"][a] = jnp.concatenate([r["r2"][q * per + a][:, :k2] for q in range(slots)], axis=1)
    everyone(r["c_own"], r["c_all"], r["c_send"], r["c_recv"])
    gy = lax.axis_size("gy")

    def place(i, carry):
        for j in range(gy):
            for x in range(n2):
                q, a = x // per, x % per
                r["r2all"][i * n2 + x, j * m2 : (j + 1) * m2, :] = jnp.concatenate(
                    [r["c_all"][(i * gy + j) * gz + k, a][:, q * k2 : (q + 1) * k2] for k in range(gz)],
                    axis=1,
                )
        return carry

    lax.fori_loop(0, lax.axis_size("gx"), place, 0)
    coarse_kernel(
        dims, r["r2all"], *level[2], *level[3], r["u2"], r["p2"],
        r["ca"], r["cb"], r["cz"], r["r3"], r["e3a"], r["e3b"], r["cbuf"],
    )
    up_kernel(
        dims, r["u2"], x1, r["e1"], *level[1], r["rhs"], r["e0"], *level[0], sol, res, r["p3"],
        r["va"], r["vb"], r["vbuf"], r["ua"], r["ub"], r["ubuf"],
    )
    row = iota((8, nz), 0)
    mine = jnp.where(row == 0, r["p0"][...], jnp.where(row == 1, r["p1"][...], r["p3"][...]))
    r["n_own"][...] = mine
    everyone(r["n_own"], r["n_all"], r["n_send"], r["n_recv"])
    total = lax.fori_loop(0, n, lambda i, t: t + r["n_all"][i], jnp.zeros((8, nz), F32))
    cells = float(nx * ny * nz * n)
    total = jnp.where(row == 2, r["p2"][...], total)
    scale = jnp.where(row == 1, 8.0 / cells, jnp.where(row == 2, 64.0 / cells, 1.0 / cells))
    norms[...] = jnp.sqrt(total * scale)


def body(data, weights):
    dims = data.shape
    nx, ny, nz = dims
    gx, gy, gz = (lax.axis_size(a) for a in AXES)
    n = gx * gy * gz
    c0, y0, l0 = nx + 2 * HX[0], ny + 8, 2 * nz
    c1, y1 = nx // 2 + 2 * HX[1], ny // 2 + 16
    N2 = (nx // 4 * gx, ny // 4 * gy, nz // 4 * gz)
    N3 = tuple(v // 2 for v in N2)
    per = -(-nx // (nz // WIDTH))
    pad2 = (N2[0] + 2,) + N2[1:]
    pad3 = (N3[0] + 2,) + N3[1:]
    own2 = (nx // 4 // 4, ny // 4, nz)
    shapes = dict(
        f_low=(per, ny, nz), f_high=(per, ny, nz), g_low=(per, ny, nz), g_high=(per, ny, nz),
        ext=(c0, y0, l0), wparts=(gz, 8, nz), y_low=(c0, 8, l0), y_high=(c0, 8, l0),
        rhs=(c0, y0, l0), e0=(c0 + 2, y0, l0), r1=(nx // 2, ny // 2, nz),
        ua=(c0 + 2, y0, l0), ub=(c0 + 2, y0, l0), gz0=(c0 + 2, y0, nz), ubuf=(c0 // 2 + 2, y0, l0),
        b_own=(nx // 4, ny // 2, nz), b_low=(nx // 4, ny // 2, nz), b_high=(nx // 4, ny // 2, nz),
        x1=(c1, y1, l0), e1=(c1 + 2, y1, l0), r2=(nx // 4, ny // 4, nz),
        va=(c1 + 2, y1, l0), vb=(c1 + 2, y1, l0), gz1=(c1 + 2, y1, nz), vbuf=(c1 // 2 + 2, y1, l0),
        c_own=own2, c_all=(n,) + own2, r2all=N2, u2=(N2[0] + 8,) + N2[1:],
        ca=pad2, cb=pad2, cz=(N2[0] + 2, N2[1], N3[2]), r3=N3, e3a=pad3, e3b=pad3,
        cbuf=(N3[0] + 2,) + N2[1:], n_own=(8, nz), n_all=(n, 8, nz),
        p0=(8, nz), p1=(8, nz), p2=(8, nz), p3=(8, nz),
    )
    scratch = {k: pltpu.VMEM(v, F32) for k, v in shapes.items()}
    for k, size in enumerate((l0, l0, N2[2], N3[2])):
        scratch["m%dh" % k] = pltpu.VMEM((size, size), BF16)
        scratch["m%dl" % k] = pltpu.VMEM((size, size), BF16)
        scratch["m%dc" % k] = pltpu.VMEM((8, size), F32)
    scratch["ah"] = scratch["al"] = pltpu.VMEM((l0, l0), BF16)
    dma = pltpu.SemaphoreType.DMA
    scratch.update(near_send=dma((14,)), near_recv=dma((14,)), w_send=dma((gz,)), w_recv=dma((gz,)))
    for k in "cn":
        scratch[k + "_send"] = dma((n,))
        scratch[k + "_recv"] = dma((n,))
    vmem = pl.BlockSpec(memory_space=pltpu.VMEM)
    sol, res, norms = pl.pallas_call(
        functools.partial(whole_kernel, tuple(scratch), dims),
        out_shape=[jax.ShapeDtypeStruct(s, F32) for s in (dims, dims, (8, nz))],
        in_specs=[vmem] * 2,
        out_specs=[vmem] * 3,
        scratch_shapes=list(scratch.values()),
        compiler_params=pltpu.CompilerParams(
            collective_id=0, has_side_effects=True, vmem_limit_bytes=60 * 1024 * 1024
        ),
    )(data, weights)
    return sol, res, norms[:4, 0]


def solution(mesh):
    in_specs = (P("gx", "gy", "gz"), P(None, "gz"))
    out_specs = (P("gx", "gy", "gz"), P("gx", "gy", "gz"), P())
    return jax.shard_map(body, mesh=mesh, in_specs=in_specs, out_specs=out_specs, check_vma=False)
```

profile of v0, /device:TPU:0, one launch (start us, length us, event | category | flops | bytes accessed | tf_op | source)
XLA Modules:
  0.0 71.5 jit_solution(14610096078795851309)
XLA Ops:
  0.6 66.8 %shard_map.49 = (f32[32,32,128]{2,1,0:T(8,128)}, f32[32,32,128]{2,1,0:T(8,128)}, f32[8,128]{1,0:T(8,128)}) custom-call(f32[32,32,128]{2,1,0:T(8,128)} %data.1, f32[8,128]{1,0:T(8,128)} %weights.1), custom_call_target="tpu_custom_call" | custom-call | tf_op jit(solution)/shard_map/pallas_call | solution.py:727
  67.5 0.0 copy-start.1
  67.5 0.7 copy-done.1
  68.2 0.6 slice_reduce_fusion
  68.8 0.0 copy-start
  68.8 1.9 %copy.7 = f32[32,32,128]{2,1,0:T(8,128)} copy(f32[32,32,128]{2,1,0:T(8,128)} %get-tuple-element.12) | data formatting | bytes 1048576
  70.7 0.0 copy-done
  70.7 0.8 %copy.8 = f32[32,32,128]{2,1,0:T(8,128)} copy(f32[32,32,128]{2,1,0:T(8,128)S(1)} %copy-done) | data formatting | bytes 1048576
Async XLA Ops:
  67.5 0.7 copy-start.1
  68.8 1.9 %copy-start = (f32[32,32,128]{2,1,0:T(8,128)S(1)}, f32[32,32,128]{2,1,0:T(8,128)}, u32[]{:S(2)}) copy-start(f32[32,32,128]{2,1,0:T(8,128)} %get-tuple-element.13) | copy-start | bytes 1572868
where the time goes:
time: 71.7 us; the launch traced here: 71.5 us
  Pallas kernels  66.8 us (93%)
  local copies, waits for them, and re-layouts  4.02 us (6%)
    pallas_call x1, Pallas kernels, body(): pl.pallas_call(functools.partial(whole_kernel, tuple(scratch), dims), out...  66.8 us
    unnamed x6, local copies, waits for them, and re-layouts  3.39 us

commit v1 on v0

--- a/solution.py
+++ b/solution.py
@@ -472,9 +472,31 @@
     return lax.axis_size("gx") * lax.axis_size("gy") * lax.axis_size("gz")
 
 
+def near_devices():
+    out = []
+    for axis, reach in (("gx", 1), ("gy", 1), ("gz", lax.axis_size("gz") - 1)):
+        n, me = lax.axis_size(axis), lax.axis_index(axis)
+        for d in range(1, reach + 1):
+            out.append((me + d < n, {axis: lax.rem(me + d, n)}))
+            out.append((me >= d, {axis: lax.rem(me + n - d, n)}))
+    return out
+
+
+def reached():
+    return lax.axis_size("gx") <= 4 and lax.axis_size("gy") <= 2
+
+
 def signal_all():
     n, me = device_count(), linear()
     barrier = pltpu.get_barrier_semaphore()
+    if reached():
+        for there, device in near_devices():
+
+            @pl.when(there)
+            def _():
+                pl.semaphore_signal(barrier, inc=1, device_id=device, device_id_type=MESH)
+
+        return
 
     def step(k, carry):
         pl.semaphore_signal(
@@ -486,6 +508,10 @@
 
 
 def wait_all():
+    if reached():
+        count = sum(there.astype(jnp.int32) for there, _ in near_devices())
+        pl.semaphore_wait(pltpu.get_barrier_semaphore(), count)
+        return
     pl.semaphore_wait(pltpu.get_barrier_semaphore(), device_count() - 1)
 
 

time: 71.7 us -> 70.3 us (0.980)
  Pallas kernels: 66.8 us -> 65.5 us
    pallas_call x1, Pallas kernels: 66.8 us -> 65.5 us  [body(): pl.pallas_call(functools.partial(whole_kernel, tuple(scratch), dims), out...]
where the time goes in v1:
time: 70.3 us; the launch traced here: 70.2 us
  Pallas kernels  65.5 us (93%)
  local copies, waits for them, and re-layouts  4.02 us (6%)
    pallas_call x1, Pallas kernels, body(): pl.pallas_call(functools.partial(whole_kernel, tuple(scratch), dims), out...  65.5 us
    unnamed x6, local copies, waits for them, and re-layouts  3.39 us

profile of v1, /device:TPU:0, one launch (start us, length us, event | category | flops | bytes accessed | tf_op | source)
XLA Modules:
  0.0 70.2 jit_solution(8224768217570899108)
XLA Ops:
  0.6 65.5 %shard_map.49 = (f32[32,32,128]{2,1,0:T(8,128)}, f32[32,32,128]{2,1,0:T(8,128)}, f32[8,128]{1,0:T(8,128)}) custom-call(f32[32,32,128]{2,1,0:T(8,128)} %data.1, f32[8,128]{1,0:T(8,128)} %weights.1), custom_call_target="tpu_custom_call" | custom-call | tf_op jit(solution)/shard_map/pallas_call | solution.py:753
  66.1 0.0 copy-start.1
  66.1 0.7 copy-done.1
  66.8 0.6 slice_reduce_fusion
  67.4 0.0 copy-start
  67.4 1.9 %copy.7 = f32[32,32,128]{2,1,0:T(8,128)} copy(f32[32,32,128]{2,1,0:T(8,128)} %get-tuple-element.12) | data formatting | bytes 1048576
  69.4 0.0 copy-done
  69.4 0.8 %copy.8 = f32[32,32,128]{2,1,0:T(8,128)} copy(f32[32,32,128]{2,1,0:T(8,128)S(1)} %copy-done) | data formatting | bytes 1048576
Async XLA Ops:
  66.1 0.7 copy-start.1
  67.4 1.9 %copy-start = (f32[32,32,128]{2,1,0:T(8,128)S(1)}, f32[32,32,128]{2,1,0:T(8,128)}, u32[]{:S(2)}) copy-start(f32[32,32,128]{2,1,0:T(8,128)} %get-tuple-element.13) | copy-start | bytes 1572868

commit v2 on v1

--- a/solution.py
+++ b/solution.py
@@ -1,4 +1,5 @@
 import functools
+import math
 import jax
 import jax.numpy as jnp
 from jax import lax
@@ -515,28 +516,58 @@
     pl.semaphore_wait(pltpu.get_barrier_semaphore(), device_count() - 1)
 
 
+def shifted(axis, d):
+    n = lax.axis_size(axis)
+    t = lax.axis_index(axis) + d
+    return jnp.where(t >= n, t - n, t)
+
+
+def arrived(buf, count, sends, recvs, k, axis):
+    part = buf.at[0:count]
+    return pltpu.make_async_remote_copy(
+        src_ref=part, dst_ref=part, send_sem=sends.at[k], recv_sem=recvs.at[k],
+        device_id={axis: shifted(axis, 1)}, device_id_type=MESH,
+    )
+
+
+def spread(block, buf, slot, sends, recvs, k, sizes):
+    for dx in range(sizes[0]):
+        for dy in range(sizes[1]):
+            for dz in range(sizes[2]):
+                if dx or dy or dz:
+                    pltpu.make_async_remote_copy(
+                        src_ref=block, dst_ref=buf.at[slot], send_sem=sends.at[k], recv_sem=recvs.at[k],
+                        device_id=(shifted("gx", dx), shifted("gy", dy), shifted("gz", dz)),
+                        device_id_type=MESH,
+                    ).start()
+
+
 def everyone(block, buf, sends, recvs):
     n, me = device_count(), linear()
-
-    def copy(k, slot):
-        return pltpu.make_async_remote_copy(
-            src_ref=block, dst_ref=buf.at[slot], send_sem=sends.at[k], recv_sem=recvs.at[k],
-            device_id=coordinates(lax.rem(me + k, n)), device_id_type=MESH,
-        )
-
-    def start(k, carry):
-        copy(k, me).start()
-        return carry
-
-    def wait(k, carry):
-        c = copy(k, lax.rem(me + n - k, n))
-        c.wait_recv()
-        c.wait_send()
-        return carry
-
-    lax.fori_loop(1, n, start, 0)
+    spread(block, buf, me, sends, recvs, 0, [lax.axis_size(a) for a in AXES])
     buf[me] = block[...]
-    lax.fori_loop(1, n, wait, 0)
+    done = arrived(buf, n - 1, sends, recvs, 0, "gz")
+    done.wait_recv()
+    return done
+
+
+def by_columns(block, buf, sends, recvs):
+    gx, gy, gz = (lax.axis_size(a) for a in AXES)
+    m, y = gx * gz, lax.axis_index("gy")
+    slot = y * m + lax.axis_index("gx") * gz + lax.axis_index("gz")
+    spread(block, buf, slot, sends, recvs, 0, (gx, 1, gz))
+    buf[slot] = block[...]
+    first = arrived(buf, m - 1, sends, recvs, 0, "gz")
+    first.wait_recv()
+    mine = buf.at[pl.ds(y * m, m)]
+    for d in range(1, gy):
+        pltpu.make_async_remote_copy(
+            src_ref=mine, dst_ref=mine, send_sem=sends.at[1], recv_sem=recvs.at[1],
+            device_id={"gy": shifted("gy", d)}, device_id_type=MESH,
+        ).start()
+    second = arrived(buf, (gy - 1) * m, sends, recvs, 1, "gy")
+    second.wait_recv()
+    return first, second
 
 
 def pack_faces(data, low, high):
@@ -679,15 +710,15 @@
     per = n2 // slots
     for a in range(per):
         r["c_own"][a] = jnp.concatenate([r["r2"][q * per + a][:, :k2] for q in range(slots)], axis=1)
-    everyone(r["c_own"], r["c_all"], r["c_send"], r["c_recv"])
-    gy = lax.axis_size("gy")
+    gathered = by_columns(r["c_own"], r["c_all"], r["c_send"], r["c_recv"])
+    gx, gy = lax.axis_size("gx"), lax.axis_size("gy")
 
     def place(i, carry):
         for j in range(gy):
             for x in range(n2):
                 q, a = x // per, x % per
                 r["r2all"][i * n2 + x, j * m2 : (j + 1) * m2, :] = jnp.concatenate(
-                    [r["c_all"][(i * gy + j) * gz + k, a][:, q * k2 : (q + 1) * k2] for k in range(gz)],
+                    [r["c_all"][(j * gx + i) * gz + k, a][:, q * k2 : (q + 1) * k2] for k in range(gz)],
                     axis=1,
                 )
         return carry
@@ -701,15 +732,19 @@
         dims, r["u2"], x1, r["e1"], *level[1], r["rhs"], r["e0"], *level[0], sol, res, r["p3"],
         r["va"], r["vb"], r["vbuf"], r["ua"], r["ub"], r["ubuf"],
     )
-    row = iota((8, nz), 0)
-    mine = jnp.where(row == 0, r["p0"][...], jnp.where(row == 1, r["p1"][...], r["p3"][...]))
+    for g in gathered:
+        g.wait_send()
+    lane = iota((1, nz), 1)
+    p0, p1, p2, p3 = (r["p%d" % k][0:1, :] for k in range(4))
+    mine = jnp.where(lane == 0, p0, jnp.where(lane == 1, p1, p3))
     r["n_own"][...] = mine
-    everyone(r["n_own"], r["n_all"], r["n_send"], r["n_recv"])
-    total = lax.fori_loop(0, n, lambda i, t: t + r["n_all"][i], jnp.zeros((8, nz), F32))
+    last = everyone(r["n_own"], r["n_all"], r["n_send"], r["n_recv"])
+    total = jnp.sum(r["n_all"][...], axis=0)
     cells = float(nx * ny * nz * n)
-    total = jnp.where(row == 2, r["p2"][...], total)
-    scale = jnp.where(row == 1, 8.0 / cells, jnp.where(row == 2, 64.0 / cells, 1.0 / cells))
+    total = jnp.where(lane == 2, p2, total)
+    scale = jnp.where(lane == 1, 8.0 / cells, jnp.where(lane == 2, 64.0 / cells, 1.0 / cells))
     norms[...] = jnp.sqrt(total * scale)
+    last.wait_send()
 
 
 def body(data, weights):
@@ -735,7 +770,7 @@
         va=(c1 + 2, y1, l0), vb=(c1 + 2, y1, l0), gz1=(c1 + 2, y1, nz), vbuf=(c1 // 2 + 2, y1, l0),
         c_own=own2, c_all=(n,) + own2, r2all=N2, u2=(N2[0] + 8,) + N2[1:],
         ca=pad2, cb=pad2, cz=(N2[0] + 2, N2[1], N3[2]), r3=N3, e3a=pad3, e3b=pad3,
-        cbuf=(N3[0] + 2,) + N2[1:], n_own=(8, nz), n_all=(n, 8, nz),
+        cbuf=(N3[0] + 2,) + N2[1:], n_own=(1, nz), n_all=(n, 1, nz),
         p0=(8, nz), p1=(8, nz), p2=(8, nz), p3=(8, nz),
     )
     scratch = {k: pltpu.VMEM(v, F32) for k, v in shapes.items()}
@@ -747,20 +782,21 @@
     dma = pltpu.SemaphoreType.DMA
     scratch.update(near_send=dma((14,)), near_recv=dma((14,)), w_send=dma((gz,)), w_recv=dma((gz,)))
     for k in "cn":
-        scratch[k + "_send"] = dma((n,))
-        scratch[k + "_recv"] = dma((n,))
+        scratch[k + "_send"] = dma((2,))
+        scratch[k + "_recv"] = dma((2,))
+    words = sum(math.prod(v) for v in shapes.values()) + 2 * l0 * l0 * 3 + N2[2] * N2[2] * 2
     vmem = pl.BlockSpec(memory_space=pltpu.VMEM)
     sol, res, norms = pl.pallas_call(
         functools.partial(whole_kernel, tuple(scratch), dims),
-        out_shape=[jax.ShapeDtypeStruct(s, F32) for s in (dims, dims, (8, nz))],
+        out_shape=[jax.ShapeDtypeStruct(s, F32) for s in (dims, dims, (1, nz))],
         in_specs=[vmem] * 2,
         out_specs=[vmem] * 3,
         scratch_shapes=list(scratch.values()),
         compiler_params=pltpu.CompilerParams(
-            collective_id=0, has_side_effects=True, vmem_limit_bytes=60 * 1024 * 1024
+            collective_id=0, has_side_effects=True, vmem_limit_bytes=4 * words + 6 * 1024 * 1024
         ),
     )(data, weights)
-    return sol, res, norms[:4, 0]
+    return sol, res, norms[0, :4]
 
 
 def solution(mesh):

time: 70.3 us -> 64.5 us (0.917)
  Pallas kernels: 65.5 us -> 59.8 us
    pallas_call x1, Pallas kernels: 65.5 us -> 59.8 us  [body(): pl.pallas_call(functools.partial(whole_kernel, tuple(scratch), dims), out...]
where the time goes in v2:
time: 64.5 us; the launch traced here: 64.3 us
  Pallas kernels  59.8 us (93%)
  local copies, waits for them, and re-layouts  3.82 us (6%)
  between operations  0.65 us (1%)
    pallas_call x1, Pallas kernels, body(): pl.pallas_call(functools.partial(whole_kernel, tuple(scratch), dims), out...  59.8 us
    unnamed x6, local copies, waits for them, and re-layouts  3.31 us

profile of v2, /device:TPU:0, one launch (start us, length us, event | category | flops | bytes accessed | tf_op | source)
XLA Modules:
  0.0 64.3 jit_solution(11126896801666509563)
XLA Ops:
  0.6 0.0 copy-start
  0.6 1.0 %copy-done = f32[32,32,128]{2,1,0:T(8,128)S(1)} copy-done((f32[32,32,128]{2,1,0:T(8,128)S(1)}, f32[32,32,128]{2,1,0:T(8,128)}, u32[]{:S(2)}) %copy-start) | copy-done | bytes 524312
  1.7 0.0 copy-start.1
  1.7 0.7 %copy-done.1 = f32[8,128]{1,0:T(8,128)S(1)} copy-done((f32[8,128]{1,0:T(8,128)S(1)}, f32[8,128]{1,0:T(8,128)}, u32[]{:S(2)}) %copy-start.1) | copy-done | bytes 4120
  2.4 59.8 %shard_map.49 = (f32[32,32,128]{2,1,0:T(8,128)S(1)}, f32[32,32,128]{2,1,0:T(8,128)S(1)}, f32[1,128]{1,0:T(1,128)S(1)}) custom-call(f32[32,32,128]{2,1,0:T(8,128)S(1)} %copy-done, f32[8,128]{1,0:T(8,128)S(1)} %copy-done.1), custom_call_target="tpu_custom_call" | custom-call | tf_op jit(solution)/shard_map/pallas_call | solution.py:789
  62.2 0.5 slice_bitcast_fusion
  62.7 0.8 %copy.7 = f32[32,32,128]{2,1,0:T(8,128)} copy(f32[32,32,128]{2,1,0:T(8,128)S(1)} %get-tuple-element.12) | data formatting | bytes 1048576
  63.5 0.8 %copy.8 = f32[32,32,128]{2,1,0:T(8,128)} copy(f32[32,32,128]{2,1,0:T(8,128)S(1)} %get-tuple-element.13) | data formatting | bytes 1048576
Async XLA Ops:
  0.6 1.0 %copy-start = (f32[32,32,128]{2,1,0:T(8,128)S(1)}, f32[32,32,128]{2,1,0:T(8,128)}, u32[]{:S(2)}) copy-start(f32[32,32,128]{2,1,0:T(8,128)} %data.1) | copy-start | bytes 1572868
  1.7 0.7 %copy-start.1 = (f32[8,128]{1,0:T(8,128)S(1)}, f32[8,128]{1,0:T(8,128)}, u32[]{:S(2)}) copy-start(f32[8,128]{1,0:T(8,128)} %weights.1) | copy-start | bytes 12292

commit v3 on v2

--- a/solution.py
+++ b/solution.py
@@ -459,6 +459,51 @@
             high[...] = jnp.zeros(high.shape, F32)
 
 
+class Star:
+    def __init__(self, src, pieces, bufs, sends, recvs, first):
+        gx, gz = lax.axis_size("gx"), lax.axis_size("gz")
+        mx, mz = lax.axis_index("gx"), lax.axis_index("gz")
+        self.moves = []
+        order = [(dx, dz) for dx in (-1, 1) for dz in (-1, 1)] + [(0, -1), (0, 1), (-1, 0), (1, 0)]
+        for k, (dx, dz) in enumerate(order):
+            to = ((mx + dx >= 0) & (mx + dx < gx) & (mz + dz >= 0) & (mz + dz < gz))
+            frm = ((mx - dx >= 0) & (mx - dx < gx) & (mz - dz >= 0) & (mz - dz < gz))
+            into = bufs[(-dx, -dz)]
+            copy = pltpu.make_async_remote_copy(
+                src_ref=src[dz].at[pieces[dx]], dst_ref=into,
+                send_sem=sends.at[first + k], recv_sem=recvs.at[first + k],
+                device_id={"gx": lax.rem(mx + dx + gx, gx), "gz": lax.rem(mz + dz + gz, gz)},
+                device_id_type=MESH,
+            )
+            self.moves.append((to, frm, copy, into))
+
+    def clear(self):
+        for _, frm, _, into in self.moves:
+
+            @pl.when(jnp.logical_not(frm))
+            def _(into=into):
+                into[...] = jnp.zeros(into.shape, F32)
+
+    def start(self):
+        for to, _, copy, _ in self.moves:
+            pl.when(to)(copy.start)
+
+    def wait(self):
+        for _, frm, copy, _ in self.moves:
+            pl.when(frm)(copy.wait_recv)
+
+    def sent(self):
+        for to, _, copy, _ in self.moves:
+            pl.when(to)(copy.wait_send)
+
+
+STAR = [(dx, dz) for dx in (-1, 0, 1) for dz in (-1, 0, 1) if dx or dz]
+
+
+def star_name(prefix, d):
+    return prefix + "mop"[d[0] + 1] + "mop"[d[1] + 1]
+
+
 def linear():
     gy, gz = lax.axis_size("gy"), lax.axis_size("gz")
     return (lax.axis_index("gx") * gy + lax.axis_index("gy")) * gz + lax.axis_index("gz")
@@ -670,39 +715,34 @@
     down_kernel(0, dims, ext, r["ah"], r["al"], *level[0], r["rhs"], r["e0"], r["r1"], r["p0"], r["ua"], r["gz0"])
     n1, m1, k1 = nx // 2, ny // 2, nz // 2
     h1 = HX[1]
-    x1, r1, half = r["x1"], r["r1"], n1 // 2
-    for a in range(half):
-        r["b_own"][a] = jnp.concatenate([r1[a][:, :k1], r1[a + half][:, :k1]], axis=1)
-    zs = Pair("gz", (r["b_own"], r["b_low"]), (r["b_own"], r["b_high"]), ns, nr, 8)
-    zs.clear(r["b_low"], r["b_high"])
-    zs.start()
-    zs.wait()
+    x1, r1, own = r["x1"], r["r1"], r["b_own"]
+    for a in range(n1 // 2):
+        own[a] = jnp.concatenate([r1[2 * a][:, :k1], r1[2 * a + 1][:, :k1]], axis=1)
+    bufs = {d: r[star_name("b_", d)] for d in STAR}
+    rim = h1 // 2
+    pieces = {-1: slice(0, rim), 0: slice(0, n1 // 2), 1: slice(n1 // 2 - rim, n1 // 2)}
+    star = Star({d: own for d in (-1, 0, 1)}, pieces, bufs, r["b_send"], r["b_recv"], 0)
+    star.start()
+    star.clear()
+    star.wait()
+    bufs[(0, 0)] = own
     blank = jnp.zeros((m1, k1), F32)
-    for x in range(n1):
-        a, part = x % half, slice((x // half) * k1, (x // half + 1) * k1)
-        x1[h1 + x, 0:m1, :] = jnp.concatenate(
-            [r1[x][:, :k1], r["b_high"][a][:, part], blank, r["b_low"][a][:, part]], axis=1
-        )
-    xs = Pair(
-        "gx",
-        (x1.at[n1 : n1 + h1, 0:m1, :], x1.at[0:h1, 0:m1, :]),
-        (x1.at[h1 : 2 * h1, 0:m1, :], x1.at[n1 + h1 : n1 + 2 * h1, 0:m1, :]),
-        ns, nr, 10,
-    )
-    xs.clear(x1.at[0:h1, 0:m1, :], x1.at[n1 + h1 : n1 + 2 * h1, 0:m1, :])
-    xs.start()
-    xs.wait()
+    for dx in (-1, 0, 1):
+        base = h1 + dx * h1 if dx < 1 else h1 + n1
+        for x in range(n1 if dx == 0 else h1):
+            a, part = x // 2, slice((x % 2) * k1, (x % 2 + 1) * k1)
+            low, mid, high = (bufs[(dx, dz)][a][:, part] for dz in (-1, 0, 1))
+            x1[base + x, 0:m1, :] = jnp.concatenate([mid, high, blank, low], axis=1)
     ys = Pair(
         "gy",
         (x1.at[:, m1 - 8 : m1, :], x1.at[:, m1 + 8 : m1 + 16, :]),
         (x1.at[:, 0:8, :], x1.at[:, m1 : m1 + 8, :]),
-        ns, nr, 12,
+        ns, nr, 8,
     )
     ys.clear(x1.at[:, m1 + 8 : m1 + 16, :], x1.at[:, m1 : m1 + 8, :])
     ys.start()
     ys.wait()
-    zs.sent()
-    xs.sent()
+    star.sent()
     ys.sent()
     down_kernel(1, dims, x1, *level[1], r["e1"], r["r2"], r["p1"], r["va"], r["gz1"])
     n2, m2, k2 = nx // 4, ny // 4, nz // 4
@@ -765,7 +805,7 @@
         ext=(c0, y0, l0), wparts=(gz, 8, nz), y_low=(c0, 8, l0), y_high=(c0, 8, l0),
         rhs=(c0, y0, l0), e0=(c0 + 2, y0, l0), r1=(nx // 2, ny // 2, nz),
         ua=(c0 + 2, y0, l0), ub=(c0 + 2, y0, l0), gz0=(c0 + 2, y0, nz), ubuf=(c0 // 2 + 2, y0, l0),
-        b_own=(nx // 4, ny // 2, nz), b_low=(nx // 4, ny // 2, nz), b_high=(nx // 4, ny // 2, nz),
+        b_own=(nx // 4, ny // 2, nz),
         x1=(c1, y1, l0), e1=(c1 + 2, y1, l0), r2=(nx // 4, ny // 4, nz),
         va=(c1 + 2, y1, l0), vb=(c1 + 2, y1, l0), gz1=(c1 + 2, y1, nz), vbuf=(c1 // 2 + 2, y1, l0),
         c_own=own2, c_all=(n,) + own2, r2all=N2, u2=(N2[0] + 8,) + N2[1:],
@@ -773,6 +813,8 @@
         cbuf=(N3[0] + 2,) + N2[1:], n_own=(1, nz), n_all=(n, 1, nz),
         p0=(8, nz), p1=(8, nz), p2=(8, nz), p3=(8, nz),
     )
+    for d in STAR:
+        shapes[star_name("b_", d)] = (HX[1] // 2 if d[0] else nx // 4, ny // 2, nz)
     scratch = {k: pltpu.VMEM(v, F32) for k, v in shapes.items()}
     for k, size in enumerate((l0, l0, N2[2], N3[2])):
         scratch["m%dh" % k] = pltpu.VMEM((size, size), BF16)
@@ -780,7 +822,8 @@
         scratch["m%dc" % k] = pltpu.VMEM((8, size), F32)
     scratch["ah"] = scratch["al"] = pltpu.VMEM((l0, l0), BF16)
     dma = pltpu.SemaphoreType.DMA
-    scratch.update(near_send=dma((14,)), near_recv=dma((14,)), w_send=dma((gz,)), w_recv=dma((gz,)))
+    scratch.update(near_send=dma((10,)), near_recv=dma((10,)), w_send=dma((gz,)), w_recv=dma((gz,)))
+    scratch.update(b_send=dma((8,)), b_recv=dma((8,)))
     for k in "cn":
         scratch[k + "_send"] = dma((2,))
         scratch[k + "_recv"] = dma((2,))

time: 64.5 us -> 60.1 us (0.932)
  Pallas kernels: 59.8 us -> 55.4 us
    pallas_call x1, Pallas kernels: 59.8 us -> 55.4 us  [body(): pl.pallas_call(functools.partial(whole_kernel, tuple(scratch), dims), out...]
where the time goes in v3:
time: 60.1 us; the launch traced here: 59.9 us
  Pallas kernels  55.4 us (92%)
  local copies, waits for them, and re-layouts  3.82 us (6%)
  between operations  0.65 us (1%)
    pallas_call x1, Pallas kernels, body(): pl.pallas_call(functools.partial(whole_kernel, tuple(scratch), dims), out...  55.4 us
    unnamed x6, local copies, waits for them, and re-layouts  3.31 us

profile of v3, /device:TPU:0, one launch (start us, length us, event | category | flops | bytes accessed | tf_op | source)
XLA Modules:
  0.0 59.9 jit_solution(13314636756204092070)
XLA Ops:
  0.6 0.0 copy-start
  0.6 1.0 %copy-done = f32[32,32,128]{2,1,0:T(8,128)S(1)} copy-done((f32[32,32,128]{2,1,0:T(8,128)S(1)}, f32[32,32,128]{2,1,0:T(8,128)}, u32[]{:S(2)}) %copy-start) | copy-done | bytes 524312
  1.7 0.0 copy-start.1
  1.7 0.7 %copy-done.1 = f32[8,128]{1,0:T(8,128)S(1)} copy-done((f32[8,128]{1,0:T(8,128)S(1)}, f32[8,128]{1,0:T(8,128)}, u32[]{:S(2)}) %copy-start.1) | copy-done | bytes 4120
  2.4 55.4 %shard_map.49 = (f32[32,32,128]{2,1,0:T(8,128)S(1)}, f32[32,32,128]{2,1,0:T(8,128)S(1)}, f32[1,128]{1,0:T(1,128)S(1)}) custom-call(f32[32,32,128]{2,1,0:T(8,128)S(1)} %copy-done, f32[8,128]{1,0:T(8,128)S(1)} %copy-done.1), custom_call_target="tpu_custom_call" | custom-call | tf_op jit(solution)/shard_map/pallas_call | solution.py:832
  57.8 0.5 slice_bitcast_fusion
  58.3 0.8 %copy.7 = f32[32,32,128]{2,1,0:T(8,128)} copy(f32[32,32,128]{2,1,0:T(8,128)S(1)} %get-tuple-element.12) | data formatting | bytes 1048576
  59.1 0.8 %copy.8 = f32[32,32,128]{2,1,0:T(8,128)} copy(f32[32,32,128]{2,1,0:T(8,128)S(1)} %get-tuple-element.13) | data formatting | bytes 1048576
Async XLA Ops:
  0.6 1.0 %copy-start = (f32[32,32,128]{2,1,0:T(8,128)S(1)}, f32[32,32,128]{2,1,0:T(8,128)}, u32[]{:S(2)}) copy-start(f32[32,32,128]{2,1,0:T(8,128)} %data.1) | copy-start | bytes 1572868
  1.7 0.7 %copy-start.1 = (f32[8,128]{1,0:T(8,128)S(1)}, f32[8,128]{1,0:T(8,128)}, u32[]{:S(2)}) copy-start(f32[8,128]{1,0:T(8,128)} %weights.1) | copy-start | bytes 12292

commit v4 on v3

--- a/solution.py
+++ b/solution.py
@@ -61,56 +61,55 @@
     return jnp.where((fine >= 0) & (fine < limit), m, 0.0).astype(F32)
 
 
-def build_matrices(nz, whole, wall, *outs):
+def build_level(level, nz, whole, wall, start, *outs):
     z0 = lax.axis_index("gz") * nz
-    for level in range(4):
-        own = nz >> level
-        total = whole >> level
-        size = 2 * nz if level < 2 else total
-        base = z0 >> level if level < 2 else 0
-
-        def place(index):
-            return cyclic(index, size, own) if level < 2 else index
-
-        g = iota((whole, size), 0) >> level
-        p = place(iota((whole, size), 1)) + base
-        pick = jnp.where(g == p, 0.5**level, 0.0).astype(F32)
-        w = lax.dot_general(
-            wall, pick, (((1,), (0,)), ((), ())),
-            preferred_element_type=F32, precision=lax.Precision.HIGHEST,
-        )
-        pr = place(iota((size, size), 0))
-        pc = place(iota((size, size), 1))
-        ok = (pr + base >= 0) & (pr + base < total) & (pc + base >= 0) & (pc + base < total)
-        diff = pr - pc
-        at = jnp.where(diff == 0, 1.0, 0.0).astype(F32)
-        for j, offset in enumerate(OFFSETS):
-            at = at + jnp.where(diff == offset, w[j : j + 1, :], 0.0)
-        at = jnp.where(ok, at, 0.0)
-        a = at.T
-        stiff = 0.25**level
-        m = lax.dot_general(
-            at, a, (((1,), (0,)), ((), ())),
-            preferred_element_type=F32, precision=lax.Precision.HIGHEST,
-        )
-        lap = jnp.where(diff == 0, 6.0, jnp.where((diff == 1) | (diff == -1), -1.0, 0.0))
-        m = m + jnp.where(ok, stiff * lap, 0.0)
-        d = jnp.sum(jnp.where(diff == 0, m, 0.0), axis=0, keepdims=True)
-        col = place(iota((1, size), 1)) + base
-        inside = (col >= 0) & (col < total)
-        safe = jnp.where(inside, d, 1.0)
-        c = jnp.where(inside, RELAX / safe, 0.0)
-        inv = jnp.where(inside, safe * (1.0 / RELAX), 0.0)
-        mh, ml = split(m * c)
-        o = outs[3 * level : 3 * level + 3]
-        o[0][...] = mh
-        o[1][...] = ml
-        o[2][0:1, :] = c
-        o[2][1:2, :] = inv
-        if level == 0:
-            ah, al = split(a)
-            outs[12][...] = ah
-            outs[13][...] = al
+    own = nz >> level
+    total = whole >> level
+    size = 2 * nz if level < 2 else total
+    base = z0 >> level if level < 2 else 0
+
+    def place(index):
+        return cyclic(index, size, own) if level < 2 else index
+
+    g = (iota((wall.shape[1], size), 0) + start) >> level
+    p = place(iota((wall.shape[1], size), 1)) + base
+    pick = jnp.where(g == p, 0.5**level, 0.0).astype(F32)
+    w = lax.dot_general(
+        wall, pick, (((1,), (0,)), ((), ())),
+        preferred_element_type=F32, precision=lax.Precision.HIGHEST,
+    )
+    pr = place(iota((size, size), 0))
+    pc = place(iota((size, size), 1))
+    ok = (pr + base >= 0) & (pr + base < total) & (pc + base >= 0) & (pc + base < total)
+    diff = pr - pc
+    at = jnp.where(diff == 0, 1.0, 0.0).astype(F32)
+    for j, offset in enumerate(OFFSETS):
+        at = at + jnp.where(diff == offset, w[j : j + 1, :], 0.0)
+    at = jnp.where(ok, at, 0.0)
+    a = at.T
+    stiff = 0.25**level
+    m = lax.dot_general(
+        at, a, (((1,), (0,)), ((), ())),
+        preferred_element_type=F32, precision=lax.Precision.HIGHEST,
+    )
+    lap = jnp.where(diff == 0, 6.0, jnp.where((diff == 1) | (diff == -1), -1.0, 0.0))
+    m = m + jnp.where(ok, stiff * lap, 0.0)
+    d = jnp.sum(jnp.where(diff == 0, m, 0.0), axis=0, keepdims=True)
+    col = place(iota((1, size), 1)) + base
+    inside = (col >= 0) & (col < total)
+    safe = jnp.where(inside, d, 1.0)
+    c = jnp.where(inside, RELAX / safe, 0.0)
+    inv = jnp.where(inside, safe * (1.0 / RELAX), 0.0)
+    mh, ml = split(m * c)
+    o = outs
+    o[0][...] = mh
+    o[1][...] = ml
+    o[2][0:1, :] = c
+    o[2][1:2, :] = inv
+    if level == 0:
+        ah, al = split(a)
+        o[3][...] = ah
+        o[4][...] = al
 
 
 def chunk_of(count, rows, most):
@@ -125,30 +124,30 @@
     mh, ml, cv = mats
     rows, size = src.shape[1], src.shape[2]
     planes = chunk_of(count, rows, most)
-    keep, lanes = own or (rows, size)
-    c = cv[0:1, 0:lanes]
-    inv = cv[1:2, 0:lanes]
-    yi = iota((rows, lanes), 0)
+    keep, lo, hi = own or (rows, 0, size)
+    c = cv[0:1, lo:hi]
+    inv = cv[1:2, lo:hi]
+    yi = iota((rows, hi - lo), 0)
 
     def step(k, carry):
         x0 = first + k * planes
         u = src[pl.ds(x0, planes), 0:keep, :]
-        um = dot3(u.reshape(planes * keep, size), mh[:, 0:lanes], ml[:, 0:lanes])
+        um = dot3(u.reshape(planes * keep, size), mh[:, lo:hi], ml[:, lo:hi])
         for p in range(planes):
             x = x0 + p
-            uc = src[x, :, 0:lanes]
+            uc = src[x, :, lo:hi]
             low = pltpu.roll(uc, 1, 0)
             high = pltpu.roll(uc, rows - 1, 0)
             if ymask is None:
                 low = jnp.where(yi == 0, 0.0, low)
                 high = jnp.where(yi == rows - 1, 0.0, high)
-            side = src[x - 1, 0:keep, 0:lanes] + src[x + 1, 0:keep, 0:lanes]
+            side = src[x - 1, 0:keep, lo:hi] + src[x + 1, 0:keep, lo:hi]
             nb = side + (low + high)[0:keep]
             if ymask is None:
                 nb = nb * stiff
             else:
-                nb = nb * (ymask[0:keep, 0:lanes] * (xmask(x) * stiff))
-            delta = c * (r_at(x)[0:keep, 0:lanes] + nb) - um[p * keep : (p + 1) * keep]
+                nb = nb * (ymask[0:keep, lo:hi] * (xmask(x) * stiff))
+            delta = c * (r_at(x)[0:keep, lo:hi] + nb) - um[p * keep : (p + 1) * keep]
             carry = emit(x, uc[0:keep], delta, inv, carry)
         return carry
 
@@ -269,6 +268,38 @@
         r_next[i] = value
 
     restrict(gz, pad, nx // 2, ry, put, lanes)
+
+
+def late_kernel(dims, ext, ah, al, mh, ml, cv, rhs, eb, ua):
+    geo = geometry(0, dims)
+    nx, ny, nz = geo["nx"], geo["ny"], geo["nz"]
+    hx = HX[0]
+    count, pad, reach = nx + 2 * hx, hx + 1, hx - 1
+    rows, size = ua.shape[1], ua.shape[2]
+    c = cv[0:1, nz:size]
+    planes = chunk_of(count, rows, 448)
+
+    def first(k, carry):
+        x0 = k * planes
+        r = dot3(ext[pl.ds(x0, planes)].reshape(planes * rows, size), ah[:, nz:size], al[:, nz:size])
+        for p in range(planes):
+            rp = r[p * rows : (p + 1) * rows]
+            rhs[x0 + p, :, nz:size] = rp
+            ua[x0 + p + 1, :, nz:size] = c * rp
+        return carry
+
+    lax.fori_loop(0, count // planes, first, 0)
+    xmask = inside_mask(geo["x0"], geo["NX"], pad)
+    ymask = y_mask(rows, size, ny, geo["y0"], geo["NY"])
+
+    def keep(x, u, delta, inv, carry):
+        eb[x, :, nz:size] = u + delta
+        return carry
+
+    sweep(
+        ua, lambda x: rhs[x - 1], keep, pad - reach, nx + 2 * reach, 1.0, (mh, ml, cv), xmask, ymask,
+        0, (rows, nz, size),
+    )
 
 
 def prolong_into(coarse_ref, coarse_first, coarse_count, pz, py, buf, error, dst, xmask):
@@ -413,14 +444,14 @@
         return carry + g * g
 
     total = sweep(
-        ua, r0_at, final, pad, nx, 1.0, mats0, xmask0, ymask0, jnp.zeros((ny, nz), F32), (ny, nz)
+        ua, r0_at, final, pad, nx, 1.0, mats0, xmask0, ymask0, jnp.zeros((ny, nz), F32), (ny, 0, nz)
     )
     part[...] = jnp.full(part.shape, jnp.sum(total), F32)
 
 
 AXES = ("gx", "gy", "gz")
 MESH = pl.DeviceIdType.MESH
-WIDTH = 40
+FIRST, WIDTH = 5 * HALF + 1, 10 * HALF
 
 
 class Pair:
@@ -460,18 +491,16 @@
 
 
 class Star:
-    def __init__(self, src, pieces, bufs, sends, recvs, first):
+    def __init__(self, moves, src, dst, sends, recvs):
         gx, gz = lax.axis_size("gx"), lax.axis_size("gz")
         mx, mz = lax.axis_index("gx"), lax.axis_index("gz")
         self.moves = []
-        order = [(dx, dz) for dx in (-1, 1) for dz in (-1, 1)] + [(0, -1), (0, 1), (-1, 0), (1, 0)]
-        for k, (dx, dz) in enumerate(order):
-            to = ((mx + dx >= 0) & (mx + dx < gx) & (mz + dz >= 0) & (mz + dz < gz))
-            frm = ((mx - dx >= 0) & (mx - dx < gx) & (mz - dz >= 0) & (mz - dz < gz))
-            into = bufs[(-dx, -dz)]
+        for k, (dx, dz) in enumerate(moves):
+            to = (mx + dx >= 0) & (mx + dx < gx) & (mz + dz >= 0) & (mz + dz < gz)
+            frm = (mx - dx >= 0) & (mx - dx < gx) & (mz - dz >= 0) & (mz - dz < gz)
+            into = dst(-dx, -dz)
             copy = pltpu.make_async_remote_copy(
-                src_ref=src[dz].at[pieces[dx]], dst_ref=into,
-                send_sem=sends.at[first + k], recv_sem=recvs.at[first + k],
+                src_ref=src(dx, dz), dst_ref=into, send_sem=sends.at[k], recv_sem=recvs.at[k],
                 device_id={"gx": lax.rem(mx + dx + gx, gx), "gz": lax.rem(mz + dz + gz, gz)},
                 device_id_type=MESH,
             )
@@ -497,7 +526,8 @@
             pl.when(to)(copy.wait_send)
 
 
-STAR = [(dx, dz) for dx in (-1, 0, 1) for dz in (-1, 0, 1) if dx or dz]
+SKEW = [(dx, dz) for dx in (-1, 1) for dz in (-1, 1)]
+STAR = SKEW + [(0, -1), (0, 1), (-1, 0), (1, 0)]
 
 
 def star_name(prefix, d):
@@ -519,17 +549,18 @@
 
 
 def near_devices():
+    sizes, me = [lax.axis_size(a) for a in AXES], [lax.axis_index(a) for a in AXES]
     out = []
-    for axis, reach in (("gx", 1), ("gy", 1), ("gz", lax.axis_size("gz") - 1)):
-        n, me = lax.axis_size(axis), lax.axis_index(axis)
-        for d in range(1, reach + 1):
-            out.append((me + d < n, {axis: lax.rem(me + d, n)}))
-            out.append((me >= d, {axis: lax.rem(me + n - d, n)}))
+    for move in [(dx, 0, dz) for dx, dz in STAR] + [(0, -1, 0), (0, 1, 0)]:
+        if all(n > 1 or d == 0 for n, d in zip(sizes, move)):
+            at = [i + d for i, d in zip(me, move)]
+            there = functools.reduce(jnp.logical_and, [(i >= 0) & (i < n) for i, n in zip(at, sizes)])
+            out.append((there, tuple(lax.rem(i + n, n) for i, n in zip(at, sizes))))
     return out
 
 
 def reached():
-    return lax.axis_size("gx") <= 4 and lax.axis_size("gy") <= 2
+    return lax.axis_size("gx") <= 4 and lax.axis_size("gy") <= 2 and lax.axis_size("gz") <= 4
 
 
 def signal_all():
@@ -603,63 +634,59 @@
     spread(block, buf, slot, sends, recvs, 0, (gx, 1, gz))
     buf[slot] = block[...]
     first = arrived(buf, m - 1, sends, recvs, 0, "gz")
-    first.wait_recv()
     mine = buf.at[pl.ds(y * m, m)]
-    for d in range(1, gy):
-        pltpu.make_async_remote_copy(
-            src_ref=mine, dst_ref=mine, send_sem=sends.at[1], recv_sem=recvs.at[1],
-            device_id={"gy": shifted("gy", d)}, device_id_type=MESH,
-        ).start()
     second = arrived(buf, (gy - 1) * m, sends, recvs, 1, "gy")
-    second.wait_recv()
-    return first, second
-
-
-def pack_faces(data, low, high):
+
+    def finish():
+        first.wait_recv()
+        for d in range(1, gy):
+            pltpu.make_async_remote_copy(
+                src_ref=mine, dst_ref=mine, send_sem=sends.at[1], recv_sem=recvs.at[1],
+                device_id={"gy": shifted("gy", d)}, device_id_type=MESH,
+            ).start()
+        second.wait_recv()
+        return first, second
+
+    return finish
+
+
+def pack_faces(data, low, high, start, stop):
     nx, ny, nz = data.shape
-    slots = nz // WIDTH
-    per = -(-nx // slots)
-    rest = jnp.zeros((ny, nz - slots * WIDTH), F32)
-    for i in range(per):
-        planes = [min(k * per + i, nx - 1) for k in range(slots)]
-        low[i] = jnp.concatenate([data[x][:, :WIDTH] for x in planes] + [rest], axis=1)
-        high[i] = jnp.concatenate([data[x][:, nz - WIDTH :] for x in planes] + [rest], axis=1)
-
-
-def unpack_faces(dims, from_low, from_high, ext, pad):
+    width = stop - start
+    slots = nz // width
+    rest = jnp.zeros((ny, nz - slots * width), F32)
+    for i in range(low.shape[0]):
+        planes = [min(i * slots + k, nx - 1) for k in range(slots)]
+        low[i] = jnp.concatenate([data[x][:, start:stop] for x in planes] + [rest], axis=1)
+        high[i] = jnp.concatenate([data[x][:, nz - stop : nz - start] for x in planes] + [rest], axis=1)
+
+
+def face_pieces(nx, hx, nz, width):
+    slots = nz // width
+    return {
+        -1: slice(0, -(-hx // slots)),
+        0: slice(0, -(-nx // slots)),
+        1: slice((nx - hx) // slots, -(-nx // slots)),
+    }
+
+
+def unpack_faces(dims, parts, widths, ext, hx):
     nx, ny, nz = dims
-    slots = nz // WIDTH
-    per = -(-nx // slots)
-    gap = jnp.zeros((ny, nz - 2 * WIDTH), F32)
-    for x in range(nx):
-        k, i = x // per, x % per
-        part = slice(k * WIDTH, (k + 1) * WIDTH)
-        ext[pad + x, 0:ny, nz:] = jnp.concatenate(
-            [from_high[i][:, part], gap, from_low[i][:, part]], axis=1
-        )
-
-
-def gather_weights(weights, parts, sends, recvs):
-    n, me = lax.axis_size("gz"), lax.axis_index("gz")
-
-    def copy(k, slot):
-        return pltpu.make_async_remote_copy(
-            src_ref=weights, dst_ref=parts.at[slot], send_sem=sends.at[k], recv_sem=recvs.at[k],
-            device_id={"gz": lax.rem(me + k, n)}, device_id_type=MESH,
-        )
-
-    for k in range(1, n):
-        copy(k, me).start()
-
-    def finish():
-        parts[me] = weights[...]
-        for k in range(1, n):
-            c = copy(k, lax.rem(me + n - k, n))
-            c.wait_recv()
-            c.wait_send()
-        return jnp.concatenate([parts[i] for i in range(n)], axis=1)
-
-    return finish
+    for dx in (-1, 0, 1):
+        source = nx - hx if dx < 0 else 0
+        target = {-1: 0, 0: hx, 1: hx + nx}[dx]
+        for i in range(nx if dx == 0 else hx):
+            ends = {}
+            for dz in (-1, 1):
+                ends[dz] = []
+                for part, width in zip(parts, widths):
+                    slots = nz // width
+                    first = (nx - hx) // slots if dx < 0 else 0
+                    x = source + i
+                    lane = x % slots * width
+                    ends[dz].append(part(dx, dz)[x // slots - first][:, lane : lane + width])
+            gap = jnp.zeros((ny, nz - 2 * sum(widths)), F32)
+            ext[target + i, 0:ny, nz:] = jnp.concatenate(ends[1] + [gap] + ends[-1][::-1], axis=1)
 
 
 def whole_kernel(names, dims, data, weights, sol, res, norms, *scratch):
@@ -668,44 +695,61 @@
     n, gz = device_count(), lax.axis_size("gz")
     ns, nr = r["near_send"], r["near_recv"]
     signal_all()
-    pack_faces(data, r["f_low"], r["f_high"])
-    ext, hx = r["ext"], HX[0]
+    pack_faces(data, r["f1_low"], r["f1_high"], 0, FIRST)
+    ext, hx, weights_row = r["ext"], HX[0], iota((8, 2 * nz), 0)
     for x in range(nx):
         ext[hx + x, 0:ny, 0:nz] = data[x]
     wait_all()
-    finish = gather_weights(weights, r["wparts"], r["w_send"], r["w_recv"])
-    faces = Pair("gz", (r["f_high"], r["g_low"]), (r["f_low"], r["g_high"]), ns, nr, 0)
-    faces.clear(r["g_low"], r["g_high"])
-    faces.start()
-
-    def x_pair(lanes, slot):
-        return Pair(
-            "gx",
-            (ext.at[nx : nx + hx, 0:ny, lanes], ext.at[0:hx, 0:ny, lanes]),
-            (ext.at[hx : 2 * hx, 0:ny, lanes], ext.at[nx + hx : nx + 2 * hx, 0:ny, lanes]),
-            ns, nr, slot,
-        )
-
-    near = x_pair(slice(0, nz), 2)
-    near.clear(ext.at[0:hx, 0:ny, :], ext.at[nx + hx : nx + 2 * hx, 0:ny, :])
+    near = Pair("gz", (weights, r["w_low"]), (weights, r["w_high"]), ns, nr, 0)
     near.start()
+    widths = (FIRST, WIDTH - FIRST)
+    pieces = [face_pieces(nx, hx, nz, w) for w in widths]
+
+    def faces(part):
+        def send(dx, dz):
+            return r["f%d_%s" % (part, "low" if dz < 0 else "high")].at[pieces[part - 1][dx]]
+
+        def take(dx, dz):
+            return r[star_name("g%d_" % part, (dx, dz))]
+
+        return send, take
+
+    send1, take1 = faces(1)
+    send2, take2 = faces(2)
+
+    def plane_send(dx, dz):
+        if dz:
+            return send1(dx, dz)
+        return data.at[0:hx] if dx < 0 else data.at[nx - hx : nx]
+
+    def plane_take(dx, dz):
+        if dz:
+            return take1(dx, dz)
+        return ext.at[0:hx, 0:ny, 0:nz] if dx < 0 else ext.at[nx + hx : nx + 2 * hx, 0:ny, 0:nz]
+
+    star = Star(STAR, plane_send, plane_take, r["s_send"], r["s_recv"])
+    star.start()
+    star.clear()
+    near.clear(r["w_low"], r["w_high"])
+    late = Star(STAR[:6], send2, take2, r["l_send"], r["l_recv"])
+    late.clear()
+    pack_faces(data, r["f2_low"], r["f2_high"], FIRST, WIDTH)
     level = [[r["m%d%s" % (k, t)] for t in "hlc"] for k in range(4)]
-    build_matrices(nz, nz * gz, finish(), *(level[0] + level[1] + level[2] + level[3]), r["ah"], r["al"])
-    faces.wait()
-    unpack_faces(dims, r["g_low"], r["g_high"], ext, hx)
-    far = x_pair(slice(nz, 2 * nz), 4)
-    far.start()
     near.wait()
-    far.wait()
-    ys = Pair("gy", (ext.at[:, ny - 8 : ny, :], r["y_low"]), (ext.at[:, 0:8, :], r["y_high"]), ns, nr, 6)
+    nearby = jnp.concatenate([r["w_low"][...], weights[...], r["w_high"][...]], axis=1)
+    start = (lax.axis_index("gz") - 1) * nz
+    build_level(0, nz, nz * gz, nearby, start, *level[0], r["ah"], r["al"])
+    star.wait()
+    late.start()
+    unpack_faces(dims, (take1,), widths[:1], ext, hx)
+    ys = Pair("gy", (ext.at[:, ny - 8 : ny, :], r["y_low"]), (ext.at[:, 0:8, :], r["y_high"]), ns, nr, 2)
     ys.clear(r["y_low"], r["y_high"])
     ys.start()
     ys.wait()
+    star.sent()
     near.sent()
-    far.sent()
-    faces.sent()
     ys.sent()
-    upper = iota((8, 2 * nz), 0) < 4
+    upper = weights_row < 4
 
     def join(x, carry):
         ext[x, ny : ny + 8, :] = jnp.where(upper, r["y_high"][x], r["y_low"][x])
@@ -720,11 +764,23 @@
         own[a] = jnp.concatenate([r1[2 * a][:, :k1], r1[2 * a + 1][:, :k1]], axis=1)
     bufs = {d: r[star_name("b_", d)] for d in STAR}
     rim = h1 // 2
-    pieces = {-1: slice(0, rim), 0: slice(0, n1 // 2), 1: slice(n1 // 2 - rim, n1 // 2)}
-    star = Star({d: own for d in (-1, 0, 1)}, pieces, bufs, r["b_send"], r["b_recv"], 0)
+    cut = {-1: slice(0, rim), 0: slice(0, n1 // 2), 1: slice(n1 // 2 - rim, n1 // 2)}
+    star = Star(
+        STAR, lambda dx, dz: own.at[cut[dx]], lambda dx, dz: bufs[(dx, dz)], r["b_send"], r["b_recv"]
+    )
     star.start()
     star.clear()
+    build_level(1, nz, nz * gz, nearby, start, *level[1])
+    late.wait()
+    unpack_faces(dims, (take1, take2), widths, ext, hx)
+    far = slice(nz, 2 * nz)
+    late_ys = Pair(
+        "gy", (ext.at[:, ny - 8 : ny, far], r["z_low"]), (ext.at[:, 0:8, far], r["z_high"]), ns, nr, 4
+    )
+    late_ys.clear(r["z_low"], r["z_high"])
+    late_ys.start()
     star.wait()
+    spread(weights, r["wparts"], lax.axis_index("gz"), r["w_send"], r["w_recv"], 0, (1, 1, gz))
     bufs[(0, 0)] = own
     blank = jnp.zeros((m1, k1), F32)
     for dx in (-1, 0, 1):
@@ -750,7 +806,22 @@
     per = n2 // slots
     for a in range(per):
         r["c_own"][a] = jnp.concatenate([r["r2"][q * per + a][:, :k2] for q in range(slots)], axis=1)
-    gathered = by_columns(r["c_own"], r["c_all"], r["c_send"], r["c_recv"])
+    finish = by_columns(r["c_own"], r["c_all"], r["c_send"], r["c_recv"])
+    late_ys.wait()
+
+    def late_join(x, carry):
+        ext[x, ny : ny + 8, far] = jnp.where(upper[:, far], r["z_high"][x], r["z_low"][x])
+        return carry
+
+    lax.fori_loop(0, nx + 2 * hx, late_join, 0)
+    late_kernel(dims, ext, r["ah"], r["al"], *level[0], r["rhs"], r["e0"], r["ua"])
+    r["wparts"][lax.axis_index("gz")] = weights[...]
+    given = arrived(r["wparts"], gz - 1, r["w_send"], r["w_recv"], 0, "gz")
+    given.wait_recv()
+    wall = jnp.concatenate([r["wparts"][i] for i in range(gz)], axis=1)
+    build_level(2, nz, nz * gz, wall, 0, *level[2])
+    build_level(3, nz, nz * gz, wall, 0, *level[3])
+    gathered = finish()
     gx, gy = lax.axis_size("gx"), lax.axis_size("gy")
 
     def place(i, carry):
@@ -772,8 +843,10 @@
         dims, r["u2"], x1, r["e1"], *level[1], r["rhs"], r["e0"], *level[0], sol, res, r["p3"],
         r["va"], r["vb"], r["vbuf"], r["ua"], r["ub"], r["ubuf"],
     )
-    for g in gathered:
+    for g in gathered + (given,):
         g.wait_send()
+    late.sent()
+    late_ys.sent()
     lane = iota((1, nz), 1)
     p0, p1, p2, p3 = (r["p%d" % k][0:1, :] for k in range(4))
     mine = jnp.where(lane == 0, p0, jnp.where(lane == 1, p1, p3))
@@ -796,13 +869,11 @@
     c1, y1 = nx // 2 + 2 * HX[1], ny // 2 + 16
     N2 = (nx // 4 * gx, ny // 4 * gy, nz // 4 * gz)
     N3 = tuple(v // 2 for v in N2)
-    per = -(-nx // (nz // WIDTH))
     pad2 = (N2[0] + 2,) + N2[1:]
     pad3 = (N3[0] + 2,) + N3[1:]
     own2 = (nx // 4 // 4, ny // 4, nz)
     shapes = dict(
-        f_low=(per, ny, nz), f_high=(per, ny, nz), g_low=(per, ny, nz), g_high=(per, ny, nz),
-        ext=(c0, y0, l0), wparts=(gz, 8, nz), y_low=(c0, 8, l0), y_high=(c0, 8, l0),
+        ext=(c0, y0, l0), wparts=(gz, 8, nz), w_low=(8, nz), w_high=(8, nz), z_low=(c0, 8, nz), z_high=(c0, 8, nz), y_low=(c0, 8, l0), y_high=(c0, 8, l0),
         rhs=(c0, y0, l0), e0=(c0 + 2, y0, l0), r1=(nx // 2, ny // 2, nz),
         ua=(c0 + 2, y0, l0), ub=(c0 + 2, y0, l0), gz0=(c0 + 2, y0, nz), ubuf=(c0 // 2 + 2, y0, l0),
         b_own=(nx // 4, ny // 2, nz),
@@ -813,6 +884,12 @@
         cbuf=(N3[0] + 2,) + N2[1:], n_own=(1, nz), n_all=(n, 1, nz),
         p0=(8, nz), p1=(8, nz), p2=(8, nz), p3=(8, nz),
     )
+    for part, width in ((1, FIRST), (2, WIDTH - FIRST)):
+        planes = {k: v.stop - v.start for k, v in face_pieces(nx, HX[0], nz, width).items()}
+        for side in ("low", "high"):
+            shapes["f%d_%s" % (part, side)] = (planes[0], ny, nz)
+        for d in STAR[:6]:
+            shapes[star_name("g%d_" % part, d)] = (planes[-d[0]], ny, nz)
     for d in STAR:
         shapes[star_name("b_", d)] = (HX[1] // 2 if d[0] else nx // 4, ny // 2, nz)
     scratch = {k: pltpu.VMEM(v, F32) for k, v in shapes.items()}
@@ -822,8 +899,10 @@
         scratch["m%dc" % k] = pltpu.VMEM((8, size), F32)
     scratch["ah"] = scratch["al"] = pltpu.VMEM((l0, l0), BF16)
     dma = pltpu.SemaphoreType.DMA
-    scratch.update(near_send=dma((10,)), near_recv=dma((10,)), w_send=dma((gz,)), w_recv=dma((gz,)))
-    scratch.update(b_send=dma((8,)), b_recv=dma((8,)))
+    scratch.update(near_send=dma((10,)), near_recv=dma((10,)), w_send=dma((1,)), w_recv=dma((1,)))
+    for k in "bsl":
+        scratch[k + "_send"] = dma((8,))
+        scratch[k + "_recv"] = dma((8,))
     for k in "cn":
         scratch[k + "_send"] = dma((2,))
         scratch[k + "_recv"] = dma((2,))

time: 60.1 us -> 57 us (0.948)
  Pallas kernels: 55.4 us -> 52.3 us
    pallas_call x1, Pallas kernels: 55.4 us -> 52.3 us  [body(): pl.pallas_call(functools.partial(whole_kernel, tuple(scratch), dims), out...]
where the time goes in v4:
time: 57 us; the launch traced here: 56.8 us
  Pallas kernels  52.3 us (92%)
  local copies, waits for them, and re-layouts  3.82 us (7%)
  between operations  0.65 us (1%)
    pallas_call x1, Pallas kernels, body(): pl.pallas_call(functools.partial(whole_kernel, tuple(scratch), dims), out...  52.3 us
    unnamed x6, local copies, waits for them, and re-layouts  3.31 us

profile of v4, /device:TPU:0, one launch (start us, length us, event | category | flops | bytes accessed | tf_op | source)
XLA Modules:
  0.0 56.8 jit_solution(6156181931520801893)
XLA Ops:
  0.6 0.0 copy-start
  0.6 1.0 %copy-done = f32[32,32,128]{2,1,0:T(8,128)S(1)} copy-done((f32[32,32,128]{2,1,0:T(8,128)S(1)}, f32[32,32,128]{2,1,0:T(8,128)}, u32[]{:S(2)}) %copy-start) | copy-done | bytes 524312
  1.7 0.0 copy-start.1
  1.7 0.7 %copy-done.1 = f32[8,128]{1,0:T(8,128)S(1)} copy-done((f32[8,128]{1,0:T(8,128)S(1)}, f32[8,128]{1,0:T(8,128)}, u32[]{:S(2)}) %copy-start.1) | copy-done | bytes 4120
  2.4 52.3 %shard_map.49 = (f32[32,32,128]{2,1,0:T(8,128)S(1)}, f32[32,32,128]{2,1,0:T(8,128)S(1)}, f32[1,128]{1,0:T(1,128)S(1)}) custom-call(f32[32,32,128]{2,1,0:T(8,128)S(1)} %copy-done, f32[8,128]{1,0:T(8,128)S(1)} %copy-done.1), custom_call_target="tpu_custom_call" | custom-call | tf_op jit(solution)/shard_map/pallas_call | solution.py:911
  54.7 0.5 slice_bitcast_fusion
  55.2 0.8 %copy.7 = f32[32,32,128]{2,1,0:T(8,128)} copy(f32[32,32,128]{2,1,0:T(8,128)S(1)} %get-tuple-element.12) | data formatting | bytes 1048576
  56.0 0.8 %copy.8 = f32[32,32,128]{2,1,0:T(8,128)} copy(f32[32,32,128]{2,1,0:T(8,128)S(1)} %get-tuple-element.13) | data formatting | bytes 1048576
Async XLA Ops:
  0.6 1.0 %copy-start = (f32[32,32,128]{2,1,0:T(8,128)S(1)}, f32[32,32,128]{2,1,0:T(8,128)}, u32[]{:S(2)}) copy-start(f32[32,32,128]{2,1,0:T(8,128)} %data.1) | copy-start | bytes 1572868
  1.7 0.7 %copy-start.1 = (f32[8,128]{1,0:T(8,128)S(1)}, f32[8,128]{1,0:T(8,128)}, u32[]{:S(2)}) copy-start(f32[8,128]{1,0:T(8,128)} %weights.1) | copy-start | bytes 12292

commit v5 on v4

--- a/solution.py
+++ b/solution.py
@@ -128,6 +128,7 @@
     c = cv[0:1, lo:hi]
     inv = cv[1:2, lo:hi]
     yi = iota((rows, hi - lo), 0)
+    cm = c if ymask is None else c * ymask[0:keep, lo:hi]
 
     def step(k, carry):
         x0 = first + k * planes
@@ -143,28 +144,29 @@
                 high = jnp.where(yi == rows - 1, 0.0, high)
             side = src[x - 1, 0:keep, lo:hi] + src[x + 1, 0:keep, lo:hi]
             nb = side + (low + high)[0:keep]
-            if ymask is None:
+            if stiff != 1.0:
                 nb = nb * stiff
-            else:
-                nb = nb * (ymask[0:keep, lo:hi] * (xmask(x) * stiff))
-            delta = c * (r_at(x)[0:keep, lo:hi] + nb) - um[p * keep : (p + 1) * keep]
+            cx = cm if ymask is None else cm * xmask(x)
+            delta = cx * (r_at(x)[0:keep, lo:hi] + nb) - um[p * keep : (p + 1) * keep]
             carry = emit(x, uc[0:keep], delta, inv, carry)
         return carry
 
     return lax.fori_loop(0, count // planes, step, init)
 
 
-def restrict(gz, first, count, ry, out, lanes):
+def restrict(gz, first, count, ry, rz, out):
     group = chunk_of(count, 1, 8)
+    rows = ry.shape[0]
 
     def step(k, carry):
         values = []
         for j in range(group):
             x = first + 2 * (k * group + j)
-            t = (gz[x - 1] + 3.0 * gz[x] + 3.0 * gz[x + 1] + gz[x + 2]) * 0.125
+            t = (gz[x - 1] + gz[x + 2] + 3.0 * (gz[x] + gz[x + 1])) * 0.125
             values.append(dot2l(ry, t))
+        z = dot2(jnp.concatenate(values, axis=0), rz)
         for j in range(group):
-            out(k * group + j, values[j])
+            out(k * group + j, z[j * rows : (j + 1) * rows])
         return carry
 
     lax.fori_loop(0, count // group, step, 0)
@@ -213,7 +215,7 @@
     reach = hx - 1 - level
     zero_planes(eb, *range(pad - reach), *range(pad + nx + reach, count + 2))
     if level == 0:
-        planes = chunk_of(count, rows, 448)
+        planes = chunk_of(count, rows, 800)
 
         def first(k, carry):
             x0 = k * planes
@@ -245,7 +247,7 @@
         return carry
 
     sweep(ua, r_at, keep, pad - reach, nx + 2 * reach, stiff, mats, xmask, ymask, 0)
-    lanes = gz.shape[2]
+    lanes = dims[2]
     fine = cyclic(iota((size, lanes), 0), size, nz)
     coarse = iota((size, lanes), 1)
     rz = jnp.where(coarse < nz // 2, restrict_matrix(fine, coarse, 0), 0.0).astype(BF16)
@@ -255,7 +257,7 @@
 
     def defect(x, u, delta, inv, carry):
         g = delta * inv
-        gz[x] = dot2(g, rz)
+        gz[x] = g
         mine = g[0:ny, 0:nz]
         return carry + mine * mine * jnp.where((x >= pad) & (x < pad + nx), 1.0, 0.0).astype(F32)
 
@@ -267,7 +269,7 @@
     def put(i, value):
         r_next[i] = value
 
-    restrict(gz, pad, nx // 2, ry, put, lanes)
+    restrict(gz, pad, nx // 2, ry, rz, put)
 
 
 def late_kernel(dims, ext, ah, al, mh, ml, cv, rhs, eb, ua):
@@ -277,7 +279,7 @@
     count, pad, reach = nx + 2 * hx, hx + 1, hx - 1
     rows, size = ua.shape[1], ua.shape[2]
     c = cv[0:1, nz:size]
-    planes = chunk_of(count, rows, 448)
+    planes = chunk_of(count, rows, 800)
 
     def first(k, carry):
         x0 = k * planes
@@ -363,7 +365,7 @@
 
     def defect(x, u, delta, inv, carry):
         g = delta * inv
-        gz[x] = dot2(g, rz)
+        gz[x] = g
         return carry + g * g
 
     total = sweep(ub, r_at, defect, 1, N2, s2, mats2, one, None, jnp.zeros((NY2, NZ2), F32))
@@ -374,7 +376,7 @@
         r3[i] = value
         e3a[i + 1] = c3v * value
 
-    restrict(gz, 1, N3, ry, put, NZ3)
+    restrict(gz, 1, N3, ry, rz, put)
     sweep(e3a, lambda x: r3[x - 1], into(e3b), 1, N3, s3, mats3, one, None, 0)
     pz = prolong_matrix(iota((NZ3, NZ2), 1), iota((NZ3, NZ2), 0), NZ2).astype(BF16)
     py = prolong_matrix(iota((NY2, NY3), 0), iota((NY2, NY3), 1), NY2).astype(BF16)
@@ -875,12 +877,12 @@
     shapes = dict(
         ext=(c0, y0, l0), wparts=(gz, 8, nz), w_low=(8, nz), w_high=(8, nz), z_low=(c0, 8, nz), z_high=(c0, 8, nz), y_low=(c0, 8, l0), y_high=(c0, 8, l0),
         rhs=(c0, y0, l0), e0=(c0 + 2, y0, l0), r1=(nx // 2, ny // 2, nz),
-        ua=(c0 + 2, y0, l0), ub=(c0 + 2, y0, l0), gz0=(c0 + 2, y0, nz), ubuf=(c0 // 2 + 2, y0, l0),
+        ua=(c0 + 2, y0, l0), ub=(c0 + 2, y0, l0), gz0=(c0 + 2, y0, l0), ubuf=(c0 // 2 + 2, y0, l0),
         b_own=(nx // 4, ny // 2, nz),
         x1=(c1, y1, l0), e1=(c1 + 2, y1, l0), r2=(nx // 4, ny // 4, nz),
-        va=(c1 + 2, y1, l0), vb=(c1 + 2, y1, l0), gz1=(c1 + 2, y1, nz), vbuf=(c1 // 2 + 2, y1, l0),
+        va=(c1 + 2, y1, l0), vb=(c1 + 2, y1, l0), gz1=(c1 + 2, y1, l0), vbuf=(c1 // 2 + 2, y1, l0),
         c_own=own2, c_all=(n,) + own2, r2all=N2, u2=(N2[0] + 8,) + N2[1:],
-        ca=pad2, cb=pad2, cz=(N2[0] + 2, N2[1], N3[2]), r3=N3, e3a=pad3, e3b=pad3,
+        ca=pad2, cb=pad2, cz=pad2, r3=N3, e3a=pad3, e3b=pad3,
         cbuf=(N3[0] + 2,) + N2[1:], n_own=(1, nz), n_all=(n, 1, nz),
         p0=(8, nz), p1=(8, nz), p2=(8, nz), p3=(8, nz),
     )

time: 57 us -> 54.9 us (0.963)
  Pallas kernels: 52.3 us -> 50.3 us
    pallas_call x1, Pallas kernels: 52.3 us -> 50.3 us  [body(): pl.pallas_call(functools.partial(whole_kernel, tuple(scratch), dims), out...]
where the time goes in v5:
time: 54.9 us; the launch traced here: 54.7 us
  Pallas kernels  50.3 us (92%)
  local copies, waits for them, and re-layouts  3.82 us (7%)
  between operations  0.65 us (1%)
    pallas_call x1, Pallas kernels, body(): pl.pallas_call(functools.partial(whole_kernel, tuple(scratch), dims), out...  50.3 us
    unnamed x6, local copies, waits for them, and re-layouts  3.31 us

profile of v5, /device:TPU:0, one launch (start us, length us, event | category | flops | bytes accessed | tf_op | source)
XLA Modules:
  0.0 54.7 jit_solution(8358716234513950946)
XLA Ops:
  0.6 0.0 copy-start
  0.6 1.0 %copy-done = f32[32,32,128]{2,1,0:T(8,128)S(1)} copy-done((f32[32,32,128]{2,1,0:T(8,128)S(1)}, f32[32,32,128]{2,1,0:T(8,128)}, u32[]{:S(2)}) %copy-start) | copy-done | bytes 524312
  1.7 0.0 copy-start.1
  1.7 0.7 %copy-done.1 = f32[8,128]{1,0:T(8,128)S(1)} copy-done((f32[8,128]{1,0:T(8,128)S(1)}, f32[8,128]{1,0:T(8,128)}, u32[]{:S(2)}) %copy-start.1) | copy-done | bytes 4120
  2.4 50.3 %shard_map.49 = (f32[32,32,128]{2,1,0:T(8,128)S(1)}, f32[32,32,128]{2,1,0:T(8,128)S(1)}, f32[1,128]{1,0:T(1,128)S(1)}) custom-call(f32[32,32,128]{2,1,0:T(8,128)S(1)} %copy-done, f32[8,128]{1,0:T(8,128)S(1)} %copy-done.1), custom_call_target="tpu_custom_call" | custom-call | tf_op jit(solution)/shard_map/pallas_call | solution.py:913
  52.6 0.5 slice_bitcast_fusion
  53.1 0.8 %copy.7 = f32[32,32,128]{2,1,0:T(8,128)} copy(f32[32,32,128]{2,1,0:T(8,128)S(1)} %get-tuple-element.12) | data formatting | bytes 1048576
  53.9 0.8 %copy.8 = f32[32,32,128]{2,1,0:T(8,128)} copy(f32[32,32,128]{2,1,0:T(8,128)S(1)} %get-tuple-element.13) | data formatting | bytes 1048576
Async XLA Ops:
  0.6 1.0 %copy-start = (f32[32,32,128]{2,1,0:T(8,128)S(1)}, f32[32,32,128]{2,1,0:T(8,128)}, u32[]{:S(2)}) copy-start(f32[32,32,128]{2,1,0:T(8,128)} %data.1) | copy-start | bytes 1572868
  1.7 0.7 %copy-start.1 = (f32[8,128]{1,0:T(8,128)S(1)}, f32[8,128]{1,0:T(8,128)}, u32[]{:S(2)}) copy-start(f32[8,128]{1,0:T(8,128)} %weights.1) | copy-start | bytes 12292

commit v6 on v5

--- a/solution.py
+++ b/solution.py
@@ -519,8 +519,9 @@
         for to, _, copy, _ in self.moves:
             pl.when(to)(copy.start)
 
-    def wait(self):
-        for _, frm, copy, _ in self.moves:
+    def wait(self, skew=None):
+        chosen = {None: self.moves, True: self.moves[:4], False: self.moves[4:]}[skew]
+        for _, frm, copy, _ in chosen:
             pl.when(frm)(copy.wait_recv)
 
     def sent(self):
@@ -652,29 +653,38 @@
     return finish
 
 
+def row_starts(nx, slots):
+    per = -(-nx // slots)
+    return [i * slots if 2 * i < per else nx - (per - i) * slots for i in range(per)]
+
+
+def find_plane(nx, slots, x, end):
+    starts = row_starts(nx, slots)
+    rows = [i for i, v in enumerate(starts) if v <= x < v + slots]
+    i = rows[-1] if end else rows[0]
+    return i, x - starts[i]
+
+
 def pack_faces(data, low, high, start, stop):
     nx, ny, nz = data.shape
     width = stop - start
     slots = nz // width
     rest = jnp.zeros((ny, nz - slots * width), F32)
     for i in range(low.shape[0]):
-        planes = [min(i * slots + k, nx - 1) for k in range(slots)]
+        planes = [row_starts(nx, slots)[i] + k for k in range(slots)]
         low[i] = jnp.concatenate([data[x][:, start:stop] for x in planes] + [rest], axis=1)
         high[i] = jnp.concatenate([data[x][:, nz - stop : nz - start] for x in planes] + [rest], axis=1)
 
 
 def face_pieces(nx, hx, nz, width):
     slots = nz // width
-    return {
-        -1: slice(0, -(-hx // slots)),
-        0: slice(0, -(-nx // slots)),
-        1: slice((nx - hx) // slots, -(-nx // slots)),
-    }
-
-
-def unpack_faces(dims, parts, widths, ext, hx):
+    per, rim = -(-nx // slots), -(-hx // slots)
+    return {-1: slice(0, rim), 0: slice(0, per), 1: slice(per - rim, per)}
+
+
+def unpack_faces(dims, parts, widths, ext, hx, sides=(-1, 0, 1)):
     nx, ny, nz = dims
-    for dx in (-1, 0, 1):
+    for dx in sides:
         source = nx - hx if dx < 0 else 0
         target = {-1: 0, 0: hx, 1: hx + nx}[dx]
         for i in range(nx if dx == 0 else hx):
@@ -683,10 +693,10 @@
                 ends[dz] = []
                 for part, width in zip(parts, widths):
                     slots = nz // width
-                    first = (nx - hx) // slots if dx < 0 else 0
-                    x = source + i
-                    lane = x % slots * width
-                    ends[dz].append(part(dx, dz)[x // slots - first][:, lane : lane + width])
+                    first = -(-nx // slots) - -(-hx // slots) if dx < 0 else 0
+                    row, lane = find_plane(nx, slots, source + i, dx < 0)
+                    lane = lane * width
+                    ends[dz].append(part(dx, dz)[row - first][:, lane : lane + width])
             gap = jnp.zeros((ny, nz - 2 * sum(widths)), F32)
             ext[target + i, 0:ny, nz:] = jnp.concatenate(ends[1] + [gap] + ends[-1][::-1], axis=1)
 
@@ -741,16 +751,31 @@
     nearby = jnp.concatenate([r["w_low"][...], weights[...], r["w_high"][...]], axis=1)
     start = (lax.axis_index("gz") - 1) * nz
     build_level(0, nz, nz * gz, nearby, start, *level[0], r["ah"], r["al"])
-    star.wait()
+    star.wait(False)
+    unpack_faces(dims, (take1,), widths[:1], ext, hx, (0,))
+
+    def y_pair(planes, slot):
+        return Pair(
+            "gy",
+            (ext.at[planes, ny - 8 : ny, :], r["y_low"].at[planes]),
+            (ext.at[planes, 0:8, :], r["y_high"].at[planes]),
+            ns, nr, slot,
+        )
+
+    ys = [y_pair(slice(a, b), k) for a, b, k in ((hx, hx + nx, 2), (0, hx, 6), (hx + nx, nx + 2 * hx, 8))]
+    ys[0].clear(r["y_low"], r["y_high"])
+    ys[0].start()
+    star.wait(True)
     late.start()
-    unpack_faces(dims, (take1,), widths[:1], ext, hx)
-    ys = Pair("gy", (ext.at[:, ny - 8 : ny, :], r["y_low"]), (ext.at[:, 0:8, :], r["y_high"]), ns, nr, 2)
-    ys.clear(r["y_low"], r["y_high"])
-    ys.start()
-    ys.wait()
+    unpack_faces(dims, (take1,), widths[:1], ext, hx, (-1, 1))
+    for y in ys[1:]:
+        y.start()
+    for y in ys:
+        y.wait()
     star.sent()
     near.sent()
-    ys.sent()
+    for y in ys:
+        y.sent()
     upper = weights_row < 4
 
     def join(x, carry):
@@ -781,21 +806,27 @@
     )
     late_ys.clear(r["z_low"], r["z_high"])
     late_ys.start()
-    star.wait()
-    spread(weights, r["wparts"], lax.axis_index("gz"), r["w_send"], r["w_recv"], 0, (1, 1, gz))
+    star.wait(False)
+    blank = jnp.zeros((m1, k1), F32)
     bufs[(0, 0)] = own
-    blank = jnp.zeros((m1, k1), F32)
-    for dx in (-1, 0, 1):
+
+    def widen(dx):
         base = h1 + dx * h1 if dx < 1 else h1 + n1
         for x in range(n1 if dx == 0 else h1):
             a, part = x // 2, slice((x % 2) * k1, (x % 2 + 1) * k1)
             low, mid, high = (bufs[(dx, dz)][a][:, part] for dz in (-1, 0, 1))
             x1[base + x, 0:m1, :] = jnp.concatenate([mid, high, blank, low], axis=1)
+
+    widen(0)
+    star.wait(True)
+    spread(weights, r["wparts"], lax.axis_index("gz"), r["w_send"], r["w_recv"], 0, (1, 1, gz))
+    widen(-1)
+    widen(1)
     ys = Pair(
         "gy",
         (x1.at[:, m1 - 8 : m1, :], x1.at[:, m1 + 8 : m1 + 16, :]),
         (x1.at[:, 0:8, :], x1.at[:, m1 : m1 + 8, :]),
-        ns, nr, 8,
+        ns, nr, 10,
     )
     ys.clear(x1.at[:, m1 + 8 : m1 + 16, :], x1.at[:, m1 : m1 + 8, :])
     ys.start()
@@ -901,7 +932,7 @@
         scratch["m%dc" % k] = pltpu.VMEM((8, size), F32)
     scratch["ah"] = scratch["al"] = pltpu.VMEM((l0, l0), BF16)
     dma = pltpu.SemaphoreType.DMA
-    scratch.update(near_send=dma((10,)), near_recv=dma((10,)), w_send=dma((1,)), w_recv=dma((1,)))
+    scratch.update(near_send=dma((12,)), near_recv=dma((12,)), w_send=dma((1,)), w_recv=dma((1,)))
     for k in "bsl":
         scratch[k + "_send"] = dma((8,))
         scratch[k + "_recv"] = dma((8,))

time: 54.9 us -> 53.6 us (0.976)
  Pallas kernels: 50.3 us -> 48.9 us
    pallas_call x1, Pallas kernels: 50.3 us -> 48.9 us  [body(): pl.pallas_call(functools.partial(whole_kernel, tuple(scratch), dims), out...]
where the time goes in v6:
time: 53.6 us; the launch traced here: 53.4 us
  Pallas kernels  48.9 us (91%)
  local copies, waits for them, and re-layouts  3.82 us (7%)
  between operations  0.65 us (1%)
    pallas_call x1, Pallas kernels, body(): pl.pallas_call(functools.partial(whole_kernel, tuple(scratch), dims), out...  48.9 us
    unnamed x6, local copies, waits for them, and re-layouts  3.31 us

profile of v6, /device:TPU:0, one launch (start us, length us, event | category | flops | bytes accessed | tf_op | source)
XLA Modules:
  0.0 53.4 jit_solution(5336679239080405255)
XLA Ops:
  0.6 0.0 copy-start
  0.6 1.0 %copy-done = f32[32,32,128]{2,1,0:T(8,128)S(1)} copy-done((f32[32,32,128]{2,1,0:T(8,128)S(1)}, f32[32,32,128]{2,1,0:T(8,128)}, u32[]{:S(2)}) %copy-start) | copy-done | bytes 524312
  1.7 0.0 copy-start.1
  1.7 0.7 %copy-done.1 = f32[8,128]{1,0:T(8,128)S(1)} copy-done((f32[8,128]{1,0:T(8,128)S(1)}, f32[8,128]{1,0:T(8,128)}, u32[]{:S(2)}) %copy-start.1) | copy-done | bytes 4120
  2.4 48.9 %shard_map.49 = (f32[32,32,128]{2,1,0:T(8,128)S(1)}, f32[32,32,128]{2,1,0:T(8,128)S(1)}, f32[1,128]{1,0:T(1,128)S(1)}) custom-call(f32[32,32,128]{2,1,0:T(8,128)S(1)} %copy-done, f32[8,128]{1,0:T(8,128)S(1)} %copy-done.1), custom_call_target="tpu_custom_call" | custom-call | tf_op jit(solution)/shard_map/pallas_call | solution.py:944
  51.3 0.5 slice_bitcast_fusion
  51.8 0.8 %copy.7 = f32[32,32,128]{2,1,0:T(8,128)} copy(f32[32,32,128]{2,1,0:T(8,128)S(1)} %get-tuple-element.12) | data formatting | bytes 1048576
  52.6 0.8 %copy.8 = f32[32,32,128]{2,1,0:T(8,128)} copy(f32[32,32,128]{2,1,0:T(8,128)S(1)} %get-tuple-element.13) | data formatting | bytes 1048576
Async XLA Ops:
  0.6 1.0 %copy-start = (f32[32,32,128]{2,1,0:T(8,128)S(1)}, f32[32,32,128]{2,1,0:T(8,128)}, u32[]{:S(2)}) copy-start(f32[32,32,128]{2,1,0:T(8,128)} %data.1) | copy-start | bytes 1572868
  1.7 0.7 %copy-start.1 = (f32[8,128]{1,0:T(8,128)S(1)}, f32[8,128]{1,0:T(8,128)}, u32[]{:S(2)}) copy-start(f32[8,128]{1,0:T(8,128)} %weights.1) | copy-start | bytes 12292
